TPU v7x, 256 devices: a whole 4x4x8 slice. The times are simulated.
256 devices in a mesh: blk: 64 (over z, y, x_hi), grp: 4 (over x_lo, core).
Axes of the slice: x: 4 (x_hi: 2, x_lo: 2; x = x_hi * 2 + x_lo), y: 4, z: 8, core: 2. Of those that a mesh axis runs over, the one named last changes fastest.
Arguments:
- start_state: float32 [512, 4096], P(('blk', 'grp')), may hold values from -6 to 6
- start_log_weight: float32 [512], P(('blk', 'grp')), may hold values from -10 to 330
- noise: bfloat16 [3, 512, 4096], P(None, ('blk', 'grp')), may hold values from -6 to 6
- first_weight: bfloat16 [14336, 4096], P('blk'), may hold values from -0.09375 to 0.09375
- second_weight: bfloat16 [14336, 4096], P('blk'), may hold values from -0.09375 to 0.09375
- third_weight: bfloat16 [14336, 4096], P('blk'), may hold values from -0.09375 to 0.09375
Outputs:
- final_state: float32 [512, 4096], P(('blk', 'grp'))
- log_weight: float32 [512], P(('blk', 'grp'))
- log_ratio: float32 [], replicated
All inputs are finite; a program needn't handle non-finite values.
Results may differ from a plain program's by a relative error of at most 0.00074.
Values may be sent and summed in bfloat16 or wider, within the bound.
A program may use at most 64 MiB of HBM per device.

v0:
```python
import math

import jax
import jax.numpy as jnp
from jax import lax
from jax.sharding import Mesh
from jax.sharding import PartitionSpec as P

BLK = ("blk_0", "blk_1", "blk_2")
BLK_GRP = ("blk_0", "blk_1", "blk_2", "grp_0", "grp_1")
GRP = ("grp_0", "grp_1")


def sent_to_all(array, axis):
    copies = jnp.broadcast_to(array, (lax.axis_size(axis), *array.shape))
    return lax.all_to_all(copies, axis, split_axis=0, concat_axis=0, tiled=True)


def joined_along(parts, dim):
    parts = jnp.moveaxis(parts, 0, dim)
    lengths = parts.shape
    return parts.reshape(*lengths[:dim], lengths[dim] * lengths[dim + 1], *lengths[dim + 2 :])


def gather_directly(array, axis, dim):
    parts = sent_to_all(array, axis)
    return joined_along(parts, dim)


def split_up(array, dim, devices):
    before, after = (array.shape[:dim], array.shape[dim + 1 :])
    return jnp.moveaxis(array.reshape(*before, devices, -1, *after), dim, 0)


def summed_on_arrival(array, axis, dim):
    parts = split_up(array, dim, lax.axis_size(axis))
    arrived = lax.all_to_all(parts, axis, split_axis=0, concat_axis=0, tiled=True)
    return arrived.sum(axis=0)


def all_in_one(array, axis):
    leaves = jax.tree.leaves(array)
    order = sorted(range(len(leaves)), key=lambda k: -leaves[k].size)
    width = (1, *leaves[order[0]].shape)[-1]
    lines = [
        jnp.pad(leaves[k].reshape(-1), (0, -leaves[k].size % width)).reshape(-1, width)
        for k in order
    ]
    both, at, found = (lax.all_gather(jnp.concatenate(lines), axis), 0, {})
    for k, line in zip(order, lines):
        section = both[:, at : at + len(line)].reshape(len(both), -1)
        found[k] = section[:, : leaves[k].size].reshape(-1, *leaves[k].shape)
        at += len(line)
    numbers = iter(range(len(leaves)))
    return jax.tree.map(lambda _: found[next(numbers)], array)


def combined_by_axis(array, axes, combine):
    for axis in axes:
        pieces = all_in_one(array, axis)
        array = jax.tree.map(lambda part: part[0], pieces)
        for k in range(1, lax.axis_size(axis)):
            array = combine(array, jax.tree.map(lambda part: part[k], pieces))
    return array


def pair_combine(first, second):
    larger = jnp.maximum(first[0], second[0])
    summed = first[1] * jnp.exp(first[0] - larger) + second[1] * jnp.exp(second[0] - larger)
    return (larger, summed)


def project_rows(piece, weights):
    contract = (((1,), (1,)), ((), ()))
    parts = [
        lax.dot_general(piece, weight, contract, preferred_element_type=jnp.float32)
        for weight in weights
    ]
    return jnp.concatenate(parts, axis=1)


def local_factors(projected, width):
    pre_a = projected[:, :width]
    pre_b = projected[:, width : 2 * width]
    pre_c = projected[:, 2 * width :]
    soft = jax.nn.softplus(pre_a)
    tan_b = jnp.tanh(pre_b)
    energy = jnp.sum(soft * tan_b * pre_c, axis=1)
    factor_a = (jax.nn.sigmoid(pre_a) * tan_b * pre_c).astype(jnp.bfloat16)
    factor_b = (soft * (1.0 - tan_b * tan_b) * pre_c).astype(jnp.bfloat16)
    factor_c = (soft * tan_b).astype(jnp.bfloat16)
    return (energy, (factor_a, factor_b, factor_c))


def back_product(factors, weights):
    total = None
    for factor, weight in zip(factors, weights):
        term = jnp.dot(factor, weight, preferred_element_type=jnp.float32)
        total = term if total is None else total + term
    return total


def per_device(start_state, start_log_weight, noise, first_weight, second_weight, third_weight):
    steps = noise.shape[0]
    own_rows = start_state.shape[0]
    width = first_weight.shape[0]
    weights = (first_weight, second_weight, third_weight)
    log_weight = start_log_weight
    state = start_state
    for step in range(steps):
        rounded = state.astype(jnp.bfloat16)
        projected = project_rows(gather_directly(rounded, BLK, 0), weights)
        energy, factors = local_factors(projected, width)
        gradient = summed_on_arrival(back_product(factors, weights), BLK, 0)
        own_energy = summed_on_arrival(energy, BLK, 0)
        log_weight = log_weight - own_energy / steps
        beta = (step + 1) / steps
        state = (
            state
            - 0.05 * (state + beta * gradient)
            + math.sqrt(0.1) * noise[step].astype(jnp.float32)
        )
    local_top = jnp.max(log_weight)
    top, total = combined_by_axis(
        (local_top, jnp.sum(jnp.exp(log_weight - local_top))), BLK_GRP, pair_combine
    )
    chain_count = own_rows * lax.axis_size(BLK) * lax.axis_size(GRP)
    log_ratio = top + jnp.log(total) - math.log(chain_count)
    return (state, log_weight, log_ratio)


def solution(mesh):
    torus = Mesh(mesh.devices.reshape(8, 4, 2, 2, 2), ("blk_0", "blk_1", "blk_2", "grp_0", "grp_1"))
    placed = (
        P(BLK_GRP, None),
        P(BLK_GRP),
        P(None, BLK_GRP, None),
        P(BLK, None),
        P(BLK, None),
        P(BLK, None),
    )
    return jax.shard_map(
        per_device,
        mesh=torus,
        in_specs=placed,
        out_specs=(P(BLK_GRP, None), P(BLK_GRP), P()),
        check_vma=False,
    )
```

profile of v0, /device:TPU:32, one launch (start us, length us, event | category | flops | bytes accessed | tf_op | source)
XLA Modules:
  0.0 450.9 jit_solution(9483340678925766633)
XLA Ops:
  0.6 0.9 convert_element_type.48
  1.6 1.0 broadcast_in_dim.9
  2.6 44.4 %all_to_all.57 = bf16[64,2,4096]{2,1,0:T(2,128)(2,1)} all-to-all(bf16[64,2,4096]{2,1,0:T(2,128)(2,1)S(1)} %broadcast_in_dim.9), channel_id=1, replica_groups=mesh['blk_0'=8,'blk_1'=4,'blk_2'=2,'grp_0'=2,'grp_1'=2] {'blk_0','blk_1'..., dimensions={0} | all-to-all | bytes 2097152 | tf_op jit(solution)/shard_map/all_to_all | solution.py:16
  47.0 1.5 reshape.167
  48.5 2.3 convolution_tanh_fusion.2
  52.6 1.0 copy-done.4
  54.1 1.9 convolution_add_fusion.4
  56.0 3.5 reshape.168
  59.5 6.2 %all-to-all-start.1 = ((f32[64,2,4096]{2,1,0:T(2,128)}), f32[64,2,4096]{2,1,0:T(2,128)}, u32[]{:S(2)}, u32[]{:S(2)}) async-start(f32[64,2,4096]{2,1,0:T(2,128)} %reshape.168), calls=%async_computation.1 | async-start | bytes 4194304 | tf_op jit(solution)/shard_map/all_to_all | solution.py:37
  65.7 51.1 %all-to-all-done.1 = f32[64,2,4096]{2,1,0:T(2,128)} async-done(((f32[64,2,4096]{2,1,0:T(2,128)}), f32[64,2,4096]{2,1,0:T(2,128)}, u32[]{:S(2)}, u32[]{:S(2)}) %all-to-all-start.1) | async-done | bytes 2097184 | tf_op jit(solution)/shard_map/all_to_all | solution.py:37
  116.7 2.2 reduce_sum.90
  119.0 1.0 broadcast_in_dim.10
  120.0 35.9 %all_to_all.58 = bf16[64,2,4096]{2,1,0:T(2,128)(2,1)} all-to-all(bf16[64,2,4096]{2,1,0:T(2,128)(2,1)S(1)} %broadcast_in_dim.10), channel_id=1, replica_groups=mesh['blk_0'=8,'blk_1'=4,'blk_2'=2,'grp_0'=2,'grp_1'=2] {'blk_0','blk_1'..., dimensions={0} | all-to-all | bytes 2097152 | tf_op jit(solution)/shard_map/all_to_all | solution.py:16
  155.9 1.5 reshape.169
  157.4 2.3 convolution_tanh_fusion.1
  161.5 1.0 copy-done.5
  163.1 1.9 convolution_add_fusion.2
  164.9 3.5 reshape.170
  168.4 57.7 %all_to_all.59 = f32[64,2,4096]{2,1,0:T(2,128)} all-to-all(f32[64,2,4096]{2,1,0:T(2,128)} %reshape.170), channel_id=1, replica_groups=mesh['blk_0'=8,'blk_1'=4,'blk_2'=2,'grp_0'=2,'grp_1'=2] {'blk_0','blk_1'..., dimensions={0} | all-to-all | bytes 4194304 | tf_op jit(solution)/shard_map/all_to_all | solution.py:37
  226.1 2.2 reduce_sum.91
  228.4 2.0 broadcast_in_dim.11
  230.4 6.1 %all-to-all-start.4 = ((bf16[64,2,4096]{2,1,0:T(2,128)(2,1)}), bf16[64,2,4096]{2,1,0:T(2,128)(2,1)S(1)}, u32[]{:S(2)}, u32[]{:S(2)}) async-start(bf16[64,2,4096]{2,1,0:T(2,128)(2,1)} %broadcast_in_dim.11), calls=%async_computation.4 | async-start | bytes 2097152 | tf_op jit(solution)/shard_map/all_to_all | solution.py:16
  236.6 0.8 all_to_all.42
  237.3 0.7 all_to_all.44
  238.1 27.6 %all-to-all-done.4 = bf16[64,2,4096]{2,1,0:T(2,128)(2,1)S(1)} async-done(((bf16[64,2,4096]{2,1,0:T(2,128)(2,1)}), bf16[64,2,4096]{2,1,0:T(2,128)(2,1)S(1)}, u32[]{:S(2)}, u32[]{:S(2)}) %all-to-all-start.4) | async-done | bytes 1048608 | tf_op jit(solution)/shard_map/all_to_all | solution.py:16
  265.7 1.0 copy-done.6
  266.7 5.9 %all-to-all-start.6 = ((f32[64,1,2]{2,1,0:T(1,128)}), f32[64,1,2]{2,1,0:T(1,128)S(1)}, u32[]{:S(2)}, u32[]{:S(2)}) async-start(f32[64,1,2]{2,1,0:T(1,128)} %bitcast.3), calls=%async_computation.6 | async-start | bytes 65536 | tf_op jit(solution)/shard_map/all_to_all | solution.py:37
  272.6 1.5 reshape.171
  274.1 2.3 convolution_tanh_fusion
  277.7 1.8 fusion.5
  279.5 4.1 all-to-all-done.6
  283.5 8.6 %all-to-all-start.7 = ((f32[64,1,2]{2,1,0:T(1,128)}), f32[64,1,2]{2,1,0:T(1,128)S(1)}, u32[]{:S(2)}, u32[]{:S(2)}) async-start(f32[64,1,2]{2,1,0:T(1,128)} %bitcast.4), calls=%async_computation.7 | async-start | bytes 65536 | tf_op jit(solution)/shard_map/all_to_all | solution.py:37
  292.2 4.0 convolution_add_fusion.1
  296.2 0.8 all_to_all.46
  296.9 6.3 %all-to-all-done.7 = f32[64,1,2]{2,1,0:T(1,128)S(1)} async-done(((f32[64,1,2]{2,1,0:T(1,128)}), f32[64,1,2]{2,1,0:T(1,128)S(1)}, u32[]{:S(2)}, u32[]{:S(2)}) %all-to-all-start.7) | async-done | bytes 544 | tf_op jit(solution)/shard_map/all_to_all | solution.py:37
  303.2 6.6 %all-to-all-start.8 = ((f32[64,1,2]{2,1,0:T(1,128)}), f32[64,1,2]{2,1,0:T(1,128)S(1)}, u32[]{:S(2)}, u32[]{:S(2)}) async-start(f32[64,1,2]{2,1,0:T(1,128)} %bitcast.5), calls=%async_computation.8 | async-start | bytes 65536 | tf_op jit(solution)/shard_map/all_to_all | solution.py:37
  309.9 3.4 convolution_add_fusion
  313.3 3.5 reshape.172
  316.8 4.0 all-to-all-done.8
  320.8 9.1 %all-to-all-start.5 = ((f32[64,2,4096]{2,1,0:T(2,128)}), f32[64,2,4096]{2,1,0:T(2,128)}, u32[]{:S(2)}, u32[]{:S(2)}) async-start(f32[64,2,4096]{2,1,0:T(2,128)} %reshape.172), calls=%async_computation.5 | async-start | bytes 4194304 | tf_op jit(solution)/shard_map/all_to_all | solution.py:37
  335.1 1.2 exponential_reduce_fusion
  336.3 1.4 fusion.18
  337.7 44.6 %all-reduce = f32[16]{0:T(128)S(1)} all-reduce(f32[16]{0:T(128)S(1)} %fusion.18), channel_id=2, replica_groups=mesh['blk_0'=8,'blk_1'=4,'blk_2'=2,'grp_0'=2,'grp_1'=2] {'blk_0'}, use_global_device_ids=true, to_apply=%add | all-reduce | flops 16 | bytes 128
  399.4 9.8 %all-reduce.1 = f32[8]{0:T(128)S(1)} all-reduce(f32[8]{0:T(128)S(1)} %fusion.19), channel_id=3, replica_groups=mesh['blk_0'=8,'blk_1'=4,'blk_2'=2,'grp_0'=2,'grp_1'=2] {'blk_1'}, use_global_device_ids=true, to_apply=%add.1 | all-reduce | flops 8 | bytes 64
  418.5 6.4 %all-reduce.2 = f32[4]{0:T(128)S(1)} all-reduce(f32[4]{0:T(128)S(1)} %fusion.20), channel_id=4, replica_groups=mesh['blk_0'=8,'blk_1'=4,'blk_2'=2,'grp_0'=2,'grp_1'=2] {'blk_2'}, use_global_device_ids=true, to_apply=%add.2 | all-reduce | flops 4 | bytes 32
  430.1 4.9 %all-reduce.3 = f32[4]{0:T(128)S(1)} all-reduce(f32[4]{0:T(128)S(1)} %fusion.21), channel_id=5, replica_groups=mesh['blk_0'=8,'blk_1'=4,'blk_2'=2,'grp_0'=2,'grp_1'=2] {'grp_0'}, use_global_device_ids=true, to_apply=%add.3 | all-reduce | flops 4 | bytes 32
  439.9 2.4 all-reduce.4
  446.9 2.2 reduce_sum.92
  (71 shorter events, 14.9 us)
Async XLA Ops:
  0.6 50.8 %copy-start = (bf16[224,4096]{1,0:T(8,128)(2,1)S(1)}, bf16[224,4096]{1,0:T(8,128)(2,1)}, u32[]{:S(2)}) copy-start(bf16[224,4096]{1,0:T(8,128)(2,1)} %param.11) | copy-start | bytes 5505028
  48.4 2.3 copy-start.1
  52.1 1.5 copy-start.4
  59.5 57.2 %all-to-all-start.1 = ((f32[64,2,4096]{2,1,0:T(2,128)}), f32[64,2,4096]{2,1,0:T(2,128)}, u32[]{:S(2)}, u32[]{:S(2)}) async-start(f32[64,2,4096]{2,1,0:T(2,128)} %reshape.168), calls=%async_computation.1 | async-start | bytes 4194304 | tf_op jit(solution)/shard_map/all_to_all | solution.py:37
  65.6 53.3 %copy-start.7 = (f32[2,4096]{1,0:T(2,128)S(1)}, f32[2,4096]{1,0:T(2,128)}, u32[]{:S(2)}) copy-start(f32[2,4096]{1,0:T(2,128)} %param.6) | copy-start | bytes 98308
  65.6 53.3 %copy-start.8 = (bf16[3,2,4096]{2,1,0:T(2,128)(2,1)S(1)}, bf16[3,2,4096]{2,1,0:T(2,128)(2,1)}, u32[]{:S(2)}) copy-start(bf16[3,2,4096]{2,1,0:T(2,128)(2,1)} %param.8) | copy-start | bytes 147460
  157.4 2.3 copy-start.2
  161.0 1.5 copy-start.5
  230.4 35.3 %all-to-all-start.4 = ((bf16[64,2,4096]{2,1,0:T(2,128)(2,1)}), bf16[64,2,4096]{2,1,0:T(2,128)(2,1)S(1)}, u32[]{:S(2)}, u32[]{:S(2)}) async-start(bf16[64,2,4096]{2,1,0:T(2,128)(2,1)} %broadcast_in_dim.11), calls=%async_computation.4 | async-start | bytes 2097152 | tf_op jit(solution)/shard_map/all_to_all | solution.py:16
  265.7 1.0 copy-start.6
  266.7 16.8 %all-to-all-start.6 = ((f32[64,1,2]{2,1,0:T(1,128)}), f32[64,1,2]{2,1,0:T(1,128)S(1)}, u32[]{:S(2)}, u32[]{:S(2)}) async-start(f32[64,1,2]{2,1,0:T(1,128)} %bitcast.3), calls=%async_computation.6 | async-start | bytes 65536 | tf_op jit(solution)/shard_map/all_to_all | solution.py:37
  274.1 2.3 copy-start.3
  283.5 19.7 %all-to-all-start.7 = ((f32[64,1,2]{2,1,0:T(1,128)}), f32[64,1,2]{2,1,0:T(1,128)S(1)}, u32[]{:S(2)}, u32[]{:S(2)}) async-start(f32[64,1,2]{2,1,0:T(1,128)} %bitcast.4), calls=%async_computation.7 | async-start | bytes 65536 | tf_op jit(solution)/shard_map/all_to_all | solution.py:37
  303.2 17.6 %all-to-all-start.8 = ((f32[64,1,2]{2,1,0:T(1,128)}), f32[64,1,2]{2,1,0:T(1,128)S(1)}, u32[]{:S(2)}, u32[]{:S(2)}) async-start(f32[64,1,2]{2,1,0:T(1,128)} %bitcast.5), calls=%async_computation.8 | async-start | bytes 65536 | tf_op jit(solution)/shard_map/all_to_all | solution.py:37
  316.8 13.1 %copy-start.15 = (u32[256]{0:T(256)S(1)}, u32[256]{0:T(256)}, u32[]{:S(2)}) copy-start(u32[256]{0:T(256)} %constant.34) | copy-start | bytes 3076
  316.8 13.7 %copy-start.14 = (u32[256]{0:T(256)S(1)}, u32[256]{0:T(256)}, u32[]{:S(2)}) copy-start(u32[256]{0:T(256)} %constant.39) | copy-start | bytes 3076
  316.8 15.6 %copy-start.13 = (u32[256]{0:T(256)S(1)}, u32[256]{0:T(256)}, u32[]{:S(2)}) copy-start(u32[256]{0:T(256)} %constant.44) | copy-start | bytes 3076
  316.8 16.8 %copy-start.12 = (u32[256]{0:T(256)S(1)}, u32[256]{0:T(256)}, u32[]{:S(2)}) copy-start(u32[256]{0:T(256)} %constant.49) | copy-start | bytes 3076
  316.8 17.7 %copy-start.9 = (f32[2]{0:T(128)S(1)}, f32[2]{0:T(128)}, u32[]{:S(2)}) copy-start(f32[2]{0:T(128)} %param.7) | copy-start | bytes 28
  316.8 101.1 %copy-start.11 = (u32[256]{0:T(256)S(1)}, u32[256]{0:T(256)}, u32[]{:S(2)}) copy-start(u32[256]{0:T(256)} %constant.54) | copy-start | bytes 3076
  320.8 126.1 %all-to-all-start.5 = ((f32[64,2,4096]{2,1,0:T(2,128)}), f32[64,2,4096]{2,1,0:T(2,128)}, u32[]{:S(2)}, u32[]{:S(2)}) async-start(f32[64,2,4096]{2,1,0:T(2,128)} %reshape.172), calls=%async_computation.5 | async-start | bytes 4194304 | tf_op jit(solution)/shard_map/all_to_all | solution.py:37
  335.1 114.7 %copy-start.10 = (f32[2]{0:T(128)}, f32[2]{0:T(128)S(1)}, u32[]{:S(2)}) copy-start(f32[2]{0:T(128)S(1)} %get-tuple-element.4) | copy-start | bytes 28
where the time goes:
time: 456 us; the launch traced here: 451 us
  blocking collectives  206 us (45%)
  waiting for transfers between devices  93 us (20%)
  starting transfers between devices  42.5 us (9%)
  between operations  40 us (9%)
  local copies, waits for them, and re-layouts  30.8 us (7%)
  matrix products  25.7 us (6%)
  other arithmetic  12.5 us (3%)
    all_to_all x2, blocking collectives, sent_to_all(): return lax.all_to_all(copies, axis, split_axis=0, concat_axis=0, tiled=True)  80.3 us
    unnamed x5, blocking collectives  68.3 us
    all_to_all x5, waiting for transfers between devices, summed_on_arrival(): lax.all_to_all(parts, axis, split_axis=0, concat_axis=0, tiled=True)  65.4 us
    all_to_all x1, blocking collectives, summed_on_arrival(): lax.all_to_all(parts, axis, split_axis=0, concat_axis=0, tiled=True)  57.7 us
    all_to_all x5, starting transfers between devices, summed_on_arrival(): lax.all_to_all(parts, axis, split_axis=0, concat_axis=0, tiled=True)  36.4 us
    all_to_all x1, waiting for transfers between devices, sent_to_all(): return lax.all_to_all(copies, axis, split_axis=0, concat_axis=0, tiled=True)  27.6 us
    dot_general x9, matrix products, back_product(): term = jnp.dot(factor, weight, preferred_element_type=jnp.float32)  15 us
    dot_general x9, matrix products, project_rows(): lax.dot_general(piece, weight, contract, preferred_element_type=jnp.float32)  10.7 us
  transfers between devices with their start and end apart: 6, of which 5 were waited for; matrix products, arithmetic and copies ran while one was open for 6% of the time, Pallas kernels for 0%

commit v1 on v0

v1 whole, which is shorter than its diff:
```python
import math

import jax
import jax.numpy as jnp
from jax import lax
from jax.experimental import pallas as pl
from jax.experimental.pallas import tpu as pltpu
from jax.sharding import Mesh
from jax.sharding import PartitionSpec as P

BLK = ("blk_0", "blk_1", "blk_2")
BLK_GRP = ("blk_0", "blk_1", "blk_2", "grp_0", "grp_1")
AXES = BLK_GRP
MESH = pl.DeviceIdType.MESH
F32 = jnp.float32
BF16 = jnp.bfloat16

NZ, NY, NX = 8, 4, 2
PEERS = NY * NX
OWN = 2
BLOCK = OWN * NZ
ROWS = PEERS * BLOCK
STEPS = 3
D = 4096
CHUNK = D // NZ
TILES = CHUNK // 128
PAD = 256
LAG_OWN, LAG_PASS, LAG_USE = 2, 4, 6


def rem(a, n):
    return lax.rem(a, n)


def kernel(
    start_ref, slw_ref, noise_ref, w1_ref, w2_ref, w3_ref,
    out_ref, lw_ref, lr_ref,
    w, s_all, g_all, rx, zs, zx, zown, state, acc, fac, ener, esum,
    ipack, iall, npack, nall, fsend, fall, e1, ex, e2, ez, e3, el,
    wsem, agx, agz, rxs, zxs, one, snd, sndg,
):
    z, y, xh, xl, core = (lax.axis_index(name) for name in AXES)
    b = y * NX + xh
    width = w1_ref.shape[0]
    mine = pl.ds(pl.multiple_of(b * BLOCK, BLOCK), BLOCK)

    def zpeer(dz):
        return (rem(z + dz, NZ), y, xh, xl, core)

    def xypeer(rel):
        dy, dx = divmod(rel, NX)
        return (z, rem(y + dy, NY), rem(xh + dx, NX), rem(xl + dx, NX), core)

    def gpeer(k):
        dl, dc = divmod(k, 2)
        return (z, y, xh, rem(xl + dl, 2), rem(core + dc, 2))

    def push(src, dst, send, recv, to):
        pltpu.make_async_remote_copy(
            src_ref=src, dst_ref=dst, send_sem=send, recv_sem=recv, device_id=to, device_id_type=MESH
        ).start()

    def arrived(ref, recv):
        pltpu.make_async_remote_copy(
            src_ref=ref, dst_ref=ref, send_sem=snd.at[0], recv_sem=recv,
            device_id=zpeer(1), device_id_type=MESH,
        ).wait_recv()

    def left(ref, send):
        pltpu.make_async_remote_copy(
            src_ref=ref, dst_ref=ref, send_sem=send, recv_sem=one.at[0],
            device_id=zpeer(1), device_id_type=MESH,
        ).wait_send()

    weights = (w1_ref, w2_ref, w3_ref)

    def weight_copy(j, k):
        cols = pl.ds(pl.multiple_of(j * CHUNK, CHUNK), CHUNK)
        return pltpu.make_async_copy(
            weights[k].at[:, cols], w.at[j, k, pl.ds(0, width), :], wsem.at[j, k]
        )

    barrier = pltpu.get_barrier_semaphore()
    greeted = [zpeer(d) for d in range(1, NZ)] + [xypeer(r) for r in range(1, PEERS)] + [gpeer(k) for k in range(1, 4)]
    for to in greeted:
        pl.semaphore_signal(barrier, inc=1, device_id=to, device_id_type=MESH)

    @pl.loop(0, NZ)
    def _(j):
        for k in range(3):
            weight_copy(j, k).start()

    for t in range(D // 128):
        v = start_ref[:, t * 128 : (t + 1) * 128]
        ipack[t : t + 1, :] = v[0:1]
        ipack[32 + t : 33 + t, :] = v[1:2]
    iall[pl.ds(pl.multiple_of(z * 64, 64), 64), :] = ipack[...]

    pl.semaphore_wait(barrier, len(greeted))

    for dz in range(1, NZ):
        push(ipack, iall.at[pl.ds(pl.multiple_of(z * 64, 64), 64), :], snd.at[0], one.at[0], zpeer(dz))

    for k in range(STEPS):
        for t in range(D // 128):
            v = noise_ref[k, :, t * 128 : (t + 1) * 128].astype(F32)
            r = (k * TILES + t % TILES) * 2
            npack[t // TILES, r : r + 2, :] = v
    nall[pl.ds(pl.multiple_of(z * 24, 8), 24), :] = npack[z]
    for dz in range(1, NZ):
        to = rem(z + dz, NZ)
        push(npack.at[to], nall.at[pl.ds(pl.multiple_of(z * 24, 8), 24), :], snd.at[1], one.at[1], zpeer(dz))

    @pl.loop(0, NZ)
    def _(j):
        for k in range(3):
            w[j, k, width:PAD, :] = jnp.zeros((PAD - width, CHUNK), BF16)

    esum[...] = jnp.zeros_like(esum)

    def spread(n, j):
        for rel in range(1, PEERS):
            push(s_all.at[n, j, mine, :], s_all.at[n, j, mine, :], snd.at[2], agx.at[n, j], xypeer(rel))

    def forward(n, j):
        arrived(s_all.at[n, j, pl.ds(0, ROWS - BLOCK), :], agx.at[n, j])
        rows = s_all[n, j]
        for k in range(3):
            term = lax.dot_general(rows, w[j, k], (((1,), (1,)), ((), ())), preferred_element_type=F32)

            @pl.when(j == 0)
            def _():
                acc[k] = term

            @pl.when(j != 0)
            def _():
                acc[k] += term

    def start_tile(t):
        lo = iall[pl.ds(t, NZ, stride=64), :]
        hi = iall[pl.ds(32 + t, NZ, stride=64), :]
        return jnp.concatenate([lo, hi], axis=0)

    arrived(iall.at[pl.ds(0, 64 * (NZ - 1)), :], one.at[0])

    @pl.loop(0, NZ)
    def _(j):
        for tt in range(TILES):
            s_all[0, j, mine, tt * 128 : (tt + 1) * 128] = start_tile(j * TILES + tt).astype(BF16)
        spread(0, j)

    for tt in range(TILES):
        state[:, tt * 128 : (tt + 1) * 128] = start_tile(z * TILES + tt)

    @pl.loop(0, NZ)
    def _(j):
        for k in range(3):
            weight_copy(j, k).wait()
        forward(0, j)

    arrived(nall.at[pl.ds(0, 24 * (NZ - 1)), :], one.at[1])

    lane = lax.broadcasted_iota(jnp.int32, (1, ROWS), 1)

    def energy_out():
        v = esum[...] / STEPS
        for i in range(OWN):
            v = v - jnp.where(lane == b * BLOCK + i * NZ + z, slw_ref[i], 0.0)
        e1[...] = jnp.broadcast_to(v, e1.shape)
        for rel in range(1, PEERS):
            push(e1, ex.at[rel - 1], snd.at[5], one.at[3], xypeer(rel))

    def energy_mid():
        arrived(ex, one.at[3])
        total = e1[...]
        for k in range(PEERS - 1):
            total = total + ex[k]
        e2[...] = total
        for dz in range(1, NZ):
            push(e2, ez.at[dz - 1], snd.at[6], one.at[4], zpeer(dz))

    def energy_end():
        arrived(ez, one.at[4])
        total = e2[...]
        for k in range(NZ - 1):
            total = total + ez[k]
        e3[...] = -total
        for k in range(1, 4):
            push(e3, el.at[k - 1], snd.at[7], one.at[5], gpeer(k))

    def step(n, carry):
        last = n == STEPS - 1

        @pl.loop(0, 4)
        def _(q):
            r = pl.ds(pl.multiple_of(q * 32, 32), 32)
            pa, pb, pc = acc[0, r], acc[1, r], acc[2, r]
            e = jnp.exp(-jnp.abs(pa))
            soft = jnp.maximum(pa, 0.0) + jnp.log1p(e)
            inv = 1.0 / (1.0 + e)
            sig = jnp.where(pa >= 0, inv, e * inv)
            tan = jnp.tanh(pb)
            fac[r, 0:PAD] = (sig * tan * pc).astype(BF16)
            fac[r, PAD : 2 * PAD] = (soft * (1.0 - tan * tan) * pc).astype(BF16)
            st = soft * tan
            fac[r, 2 * PAD :] = st.astype(BF16)
            en = st * pc
            ener[r, :] = en[:, :128] + en[:, 128:]

        @pl.loop(0, NZ)
        def _(j):
            g = jnp.dot(fac[...], w[j].reshape(3 * PAD, CHUNK), preferred_element_type=F32)
            g_all[n, j] = g.astype(BF16)
            for rel in range(1, PEERS):
                dy, dx = divmod(rel, NX)
                to = rem(y + dy, NY) * NX + rem(xh + dx, NX)
                rows = pl.ds(pl.multiple_of(to * BLOCK, BLOCK), BLOCK)
                push(g_all.at[n, j, rows, :], rx.at[n, j, rel - 1], sndg.at[n], rxs.at[n, j], xypeer(rel))

        esum[...] += jnp.sum(ener[...].T, axis=0, keepdims=True)

        @pl.when(last)
        def _():
            energy_out()
            energy_mid()

        def mix(it, carry):
            @pl.when(it < NZ)
            def _():
                arrived(rx.at[n, it], rxs.at[n, it])
                total = g_all[n, it, mine, :].astype(F32)
                for k in range(PEERS - 1):
                    total = total + rx[n, it, k].astype(F32)

                @pl.when(it == z)
                def _():
                    zown[...] = total

                @pl.when(it != z)
                def _():
                    zs[n, it] = total.astype(BF16)
                    dz = rem(it - z + NZ, NZ)
                    push(zs.at[n, it], zx.at[n, dz - 1], snd.at[3], zxs.at[n], (it, y, xh, xl, core))

            @pl.when(it - LAG_OWN == z)
            def _():
                arrived(zx.at[n], zxs.at[n])
                grad = zown[...]
                for k in range(NZ - 1):
                    grad = grad + zx[n, k].astype(F32)
                beta = (n + 1).astype(F32) / STEPS
                news = []
                for tt in range(TILES):
                    cols = slice(tt * 128, (tt + 1) * 128)
                    row = (n * TILES + tt) * 2
                    extra = jnp.concatenate(
                        [nall[pl.ds(row, NZ, stride=24), :], nall[pl.ds(row + 1, NZ, stride=24), :]], axis=0
                    )
                    old = state[:, cols]
                    new = old - 0.05 * (old + beta * grad[:, cols]) + math.sqrt(0.1) * extra
                    state[:, cols] = new

                @pl.when(jnp.logical_not(last))
                def _():
                    s_all[n + 1, z, mine, :] = state[...].astype(BF16)
                    for dz in range(1, NZ):
                        push(s_all.at[n + 1, z, mine, :], s_all.at[n + 1, z, mine, :], snd.at[4], agz.at[n, z], zpeer(dz))
                    spread(n + 1, z)

            @pl.when(jnp.logical_not(last))
            def _():
                jp = it - LAG_PASS

                @pl.when((jp >= 0) & (jp < NZ) & (jp != z))
                def _():
                    arrived(s_all.at[n + 1, jp, mine, :], agz.at[n, jp])
                    spread(n + 1, jp)

                ju = it - LAG_USE

                @pl.when((ju >= 0) & (ju < NZ))
                def _():
                    forward(n + 1, ju)

            return carry

        lax.fori_loop(0, jnp.where(last, NZ + LAG_OWN, NZ + LAG_USE), mix, 0)
        return carry

    lax.fori_loop(0, STEPS, step, 0)

    for i in range(OWN):
        for tt in range(TILES):
            fsend[pl.ds(i * TILES + tt, NZ, stride=8), :] = state[i * NZ : (i + 1) * NZ, tt * 128 : (tt + 1) * 128]
    for dz in range(1, NZ):
        to = rem(z + dz, NZ)
        push(fsend.at[pl.ds(pl.multiple_of(to * 8, 8), 8), :], fall.at[z], snd.at[8], one.at[2], zpeer(dz))
    fall[z] = fsend[pl.ds(pl.multiple_of(z * 8, 8), 8), :]
    energy_end()
    arrived(el, one.at[5])
    lws = [e3[0:1]] + [el[k, 0:1] for k in range(3)]
    top = jnp.max(jnp.maximum(jnp.maximum(lws[0], lws[1]), jnp.maximum(lws[2], lws[3])))
    total = jnp.sum(sum(jnp.exp(v - top) for v in lws), axis=1, keepdims=True)
    chains = ROWS * 4
    lr_ref[0] = jnp.max(top + jnp.log(total) - math.log(chains))
    for i in range(OWN):
        lw_ref[i] = jnp.sum(jnp.where(lane == b * BLOCK + i * NZ + z, lws[0], 0.0))
    arrived(fall.at[pl.ds(0, NZ - 1)], one.at[2])
    for zz in range(NZ):
        for i in range(OWN):
            for tt in range(TILES):
                c = (zz * TILES + tt) * 128
                out_ref[i : i + 1, c : c + 128] = fall[zz, i * TILES + tt : i * TILES + tt + 1, :]

    left(iall.at[pl.ds(0, 64 * (NZ - 1)), :], snd.at[0])
    left(npack.at[pl.ds(0, NZ - 1)], snd.at[1])
    left(s_all.at[:, :, pl.ds(0, ROWS - BLOCK), :], snd.at[2])
    left(zs.at[:, pl.ds(0, NZ - 1)], snd.at[3])
    left(zx.at[pl.ds(0, STEPS - 1)], snd.at[4])
    left(ex, snd.at[5])
    left(ez, snd.at[6])
    left(el, snd.at[7])
    left(fall.at[pl.ds(0, NZ - 1)], snd.at[8])
    for n in range(STEPS):
        left(g_all.at[n, :, pl.ds(0, ROWS - BLOCK), :], sndg.at[n])


def per_device(start_state, start_log_weight, noise, first_weight, second_weight, third_weight):
    vmem = pl.BlockSpec(memory_space=pltpu.VMEM)
    smem = pl.BlockSpec(memory_space=pltpu.SMEM)
    hbm = pl.BlockSpec(memory_space=pl.ANY)
    tile = (8, 128)
    state, log_weight, log_ratio = pl.pallas_call(
        kernel,
        out_shape=(
            jax.ShapeDtypeStruct((OWN, D), F32),
            jax.ShapeDtypeStruct((OWN,), F32),
            jax.ShapeDtypeStruct((1,), F32),
        ),
        in_specs=[vmem, smem, vmem, hbm, hbm, hbm],
        out_specs=(vmem, smem, smem),
        scratch_shapes=[
            pltpu.VMEM((NZ, 3, PAD, CHUNK), BF16),
            pltpu.VMEM((STEPS, NZ, ROWS, CHUNK), BF16),
            pltpu.VMEM((STEPS, NZ, ROWS, CHUNK), BF16),
            pltpu.VMEM((STEPS, NZ, PEERS - 1, BLOCK, CHUNK), BF16),
            pltpu.VMEM((STEPS, NZ, BLOCK, CHUNK), BF16),
            pltpu.VMEM((STEPS, NZ - 1, BLOCK, CHUNK), BF16),
            pltpu.VMEM((BLOCK, CHUNK), F32),
            pltpu.VMEM((BLOCK, CHUNK), F32),
            pltpu.VMEM((3, ROWS, PAD), F32),
            pltpu.VMEM((ROWS, 3 * PAD), BF16),
            pltpu.VMEM((ROWS, 128), F32),
            pltpu.VMEM((1, ROWS), F32),
            pltpu.VMEM((64, 128), F32),
            pltpu.VMEM((64 * NZ, 128), F32),
            pltpu.VMEM((NZ, 24, 128), F32),
            pltpu.VMEM((24 * NZ, 128), F32),
            pltpu.VMEM((64, 128), F32),
            pltpu.VMEM((NZ, 8, 128), F32),
            pltpu.VMEM(tile, F32),
            pltpu.VMEM((PEERS - 1, *tile), F32),
            pltpu.VMEM(tile, F32),
            pltpu.VMEM((NZ - 1, *tile), F32),
            pltpu.VMEM(tile, F32),
            pltpu.VMEM((3, *tile), F32),
            pltpu.SemaphoreType.DMA((NZ, 3)),
            pltpu.SemaphoreType.DMA((STEPS, NZ)),
            pltpu.SemaphoreType.DMA((STEPS - 1, NZ)),
            pltpu.SemaphoreType.DMA((STEPS, NZ)),
            pltpu.SemaphoreType.DMA((STEPS,)),
            pltpu.SemaphoreType.DMA((6,)),
            pltpu.SemaphoreType.DMA((9,)),
            pltpu.SemaphoreType.DMA((STEPS,)),
        ],
        compiler_params=pltpu.CompilerParams(
            collective_id=0, has_side_effects=True, vmem_limit_bytes=48 << 20
        ),
    )(start_state, start_log_weight, noise, first_weight, second_weight, third_weight)
    return state, log_weight, log_ratio[0]


def solution(mesh):
    torus = Mesh(mesh.devices.reshape(8, 4, 2, 2, 2), AXES)
    placed = (
        P(BLK_GRP, None),
        P(BLK_GRP),
        P(None, BLK_GRP, None),
        P(BLK, None),
        P(BLK, None),
        P(BLK, None),
    )
    return jax.shard_map(
        per_device,
        mesh=torus,
        in_specs=placed,
        out_specs=(P(BLK_GRP, None), P(BLK_GRP), P()),
        check_vma=False,
    )
```

time: 456 us -> 144 us (0.32); the launches traced: 451 us -> 144 us
  blocking collectives: 206 us -> 0 us
  Pallas kernels: 0 us -> 133 us
  waiting for transfers between devices: 93 us -> 0 us
  starting transfers between devices: 42.5 us -> 0 us
  between operations: 40 us -> 2.47 us
  matrix products: 25.7 us -> 0 us
  local copies, waits for them, and re-layouts: 30.8 us -> 7.83 us
  other arithmetic: 12.5 us -> 0 us
    all_to_all x3 -> x0, blocking collectives: 138 us -> none  [the longest x2 80.3 us: sent_to_all(): return lax.all_to_all(copies, axis, split_axis=0, concat_axis=0, tiled=True)]
    pallas_call x0 -> x1, Pallas kernels: none -> 133 us  [per_device(): pl.pallas_call(kernel, out_shape=(jax.ShapeDtypeStruct((OWN, D), F32), ja...]
    all_to_all x6 -> x0, waiting for transfers between devices: 93 us -> none  [the longest x5 65.4 us: summed_on_arrival(): lax.all_to_all(parts, axis, split_axis=0, concat_axis=0, tiled=True)]
    unnamed x5 -> x0, blocking collectives: 68.3 us -> none
    all_to_all x6 -> x0, starting transfers between devices: 42.5 us -> none  [the longest x5 36.4 us: summed_on_arrival(): lax.all_to_all(parts, axis, split_axis=0, concat_axis=0, tiled=True)]
    dot_general x18 -> x0, matrix products: 25.7 us -> none  [the longest x9 15 us: back_product(): term = jnp.dot(factor, weight, preferred_element_type=jnp.float32)]
    reshape x6 -> x0, local copies, waits for them, and re-layouts: 14.9 us -> none  [the longest x3 10.5 us: split_up(): return jnp.moveaxis(array.reshape(*before, devices, -1, *after), dim, 0)]
    reduce_sum x7 -> x0, other arithmetic: 8.17 us -> none  [the longest x6 6.93 us: summed_on_arrival(): return arrived.sum(axis=0)]
  transfers between devices with their start and end apart: 6 -> 0, of which waited for: 5 -> 0; matrix products, arithmetic and copies ran while one was open for 6% -> 0% of each run, Pallas kernels for 0% -> 0%
where the time goes in v1:
time: 144 us
  Pallas kernels  133 us (92%)
  local copies, waits for them, and re-layouts  7.83 us (5%)
  between operations  2.47 us (2%)
    pallas_call x1, Pallas kernels, per_device(): pl.pallas_call(kernel, out_shape=(jax.ShapeDtypeStruct((OWN, D), F32), ja...  133 us
    unnamed x14, local copies, waits for them, and re-layouts  7.83 us

profile of v1, /device:TPU:32, one launch (start us, length us, event | category | flops | bytes accessed | tf_op | source)
XLA Modules:
  0.0 143.7 jit_solution(940702491163022366)
XLA Ops:
  0.6 0.0 copy-start
  0.6 1.5 %copy-done = bf16[224,4096]{1,0:T(8,128)(2,1)S(1)} copy-done((bf16[224,4096]{1,0:T(8,128)(2,1)S(1)}, bf16[224,4096]{1,0:T(8,128)(2,1)}, u32[]{:S(2)}) %copy-start) | copy-done | bytes 1835032
  2.1 0.0 copy-start.1
  2.1 1.5 %copy-done.1 = bf16[224,4096]{1,0:T(8,128)(2,1)S(1)} copy-done((bf16[224,4096]{1,0:T(8,128)(2,1)S(1)}, bf16[224,4096]{1,0:T(8,128)(2,1)}, u32[]{:S(2)}) %copy-start.1) | copy-done | bytes 1835032
  3.6 0.0 copy-start.2
  3.6 1.5 %copy-done.2 = bf16[224,4096]{1,0:T(8,128)(2,1)S(1)} copy-done((bf16[224,4096]{1,0:T(8,128)(2,1)S(1)}, bf16[224,4096]{1,0:T(8,128)(2,1)}, u32[]{:S(2)}) %copy-start.2) | copy-done | bytes 1835032
  5.1 0.0 copy-start.3
  5.1 0.8 copy-done.3
  5.9 0.0 copy-start.4
  5.9 0.8 copy-done.4
  6.7 0.0 copy-start.5
  6.7 0.7 copy-done.5
  7.3 133.4 %shard_map.85 = (f32[2,4096]{1,0:T(2,128)S(1)}, f32[2]{0:T(128)S(1)}, f32[1]{0:T(128)}) custom-call(f32[2,4096]{1,0:T(2,128)S(1)} %copy-done.4, f32[2]{0:T(128)S(1)} %copy-done.5, bf16[3,2,4096]{2,1,0:T(2,128)(2,1)S(1)} %copy-done.3, bf16[224,4096]{1,0:T(8,128)(2,1)S(1)} %copy-done, bf16[224,4096]{1,0:T(8,128)(2,1)S(1)} %copy-done.1, ...), custom_call_target="tpu_custom_call" | custom-call | tf_op jit(solution)/shard_map/pallas_call | solution.py:333
  140.8 0.6 copy.12
  141.4 0.5 copy.13
Async XLA Ops:
  0.6 1.5 %copy-start = (bf16[224,4096]{1,0:T(8,128)(2,1)S(1)}, bf16[224,4096]{1,0:T(8,128)(2,1)}, u32[]{:S(2)}) copy-start(bf16[224,4096]{1,0:T(8,128)(2,1)} %w1_ref.1) | copy-start | bytes 5505028
  2.1 1.5 %copy-start.1 = (bf16[224,4096]{1,0:T(8,128)(2,1)S(1)}, bf16[224,4096]{1,0:T(8,128)(2,1)}, u32[]{:S(2)}) copy-start(bf16[224,4096]{1,0:T(8,128)(2,1)} %w2_ref.1) | copy-start | bytes 5505028
  3.6 1.5 %copy-start.2 = (bf16[224,4096]{1,0:T(8,128)(2,1)S(1)}, bf16[224,4096]{1,0:T(8,128)(2,1)}, u32[]{:S(2)}) copy-start(bf16[224,4096]{1,0:T(8,128)(2,1)} %w3_ref.1) | copy-start | bytes 5505028
  5.1 0.8 copy-start.3
  5.9 0.8 copy-start.4
  6.7 0.7 copy-start.5

commit v2 on v0

v2 whole, which is shorter than its diff:
```python
import math

import jax
import jax.numpy as jnp
from jax import lax
from jax.experimental import pallas as pl
from jax.experimental.pallas import tpu as pltpu
from jax.sharding import Mesh
from jax.sharding import PartitionSpec as P

BLK = ("blk_0", "blk_1", "blk_2")
BLK_GRP = ("blk_0", "blk_1", "blk_2", "grp_0", "grp_1")
AXES = BLK_GRP
MESH = pl.DeviceIdType.MESH
F32 = jnp.float32
BF16 = jnp.bfloat16

NZ, NY, NX = 8, 4, 2
OWN = 2
BLOCK = NX * NZ
ROWS = NY * BLOCK
STEPS = 3
PHASES = STEPS * OWN
D = 4096
COLS = D // (NX * NZ)
PART = 4
SIDE = D // (NX * PART)
CHUNK = NX * SIDE
PAIR = SIDE // COLS
TILES = COLS // 128
SRC = NX * NZ
PAD = 256
PEERS = NY * NX - 1
SENT = CHUNK * PEERS // (PEERS + 1)


def rem(a, n):
    return lax.rem(a, n)


def at(start, size):
    return pl.ds(pl.multiple_of(start, size), size)


def kernel(
    start_hbm, slw_hbm, noise_hbm, w1_ref, w2_ref, w3_ref,
    out_ref, lw_ref, lr_ref,
    start_ref, slw_ref, noise_ref,
    w, s_all, g_all, rx, zs, zx, zown, state, acc, fac, esum,
    ipack, iall, conv, wide, dpack, dall, fsend, fall, e1, ex, e2, ez, e3, el,
    insem, wsem, agx, agz, rxs, zxs, one, snd, sndg,
):
    z, y, xh, xl, core = (lax.axis_index(name) for name in AXES)
    width = w1_ref.shape[0]
    rows_y = at(y * BLOCK, BLOCK)
    side = at(xh * SIDE, SIDE)
    slot = xh * NZ + z

    def zpeer(dz):
        return (rem(z + dz, NZ), y, xh, xl, core)

    def xypeer(rel):
        dy, dx = divmod(rel, NX)
        return (z, rem(y + dy, NY), rem(xh + dx, NX), rem(xl + dx, NX), core)

    def zxpeer(k):
        dz, dx = divmod(k, NX)
        return (rem(z + dz, NZ), y, rem(xh + dx, NX), rem(xl + dx, NX), core)

    def gpeer(k):
        dl, dc = divmod(k, 2)
        return (z, y, xh, rem(xl + dl, 2), rem(core + dc, 2))

    def push(src, dst, send, recv, to):
        pltpu.make_async_remote_copy(
            src_ref=src, dst_ref=dst, send_sem=send, recv_sem=recv, device_id=to, device_id_type=MESH
        ).start()

    def arrived(ref, recv):
        pltpu.make_async_remote_copy(
            src_ref=ref, dst_ref=ref, send_sem=snd.at[0], recv_sem=recv,
            device_id=zpeer(1), device_id_type=MESH,
        ).wait_recv()

    def left(ref, send):
        pltpu.make_async_remote_copy(
            src_ref=ref, dst_ref=ref, send_sem=send, recv_sem=one.at[0],
            device_id=zpeer(1), device_id_type=MESH,
        ).wait_send()

    inputs = (
        pltpu.make_async_copy(start_hbm, start_ref, insem.at[0]),
        pltpu.make_async_copy(noise_hbm, noise_ref, insem.at[1]),
        pltpu.make_async_copy(slw_hbm, slw_ref, insem.at[2]),
    )
    for copy in inputs:
        copy.start()

    barrier = pltpu.get_barrier_semaphore()
    greeted = (
        [zxpeer(k) for k in range(1, SRC)]
        + [xypeer(r) for r in range(2, PEERS + 1)]
        + [gpeer(k) for k in range(1, 4)]
    )
    for to in greeted:
        pl.semaphore_signal(barrier, inc=1, device_id=to, device_id_type=MESH)

    weights = (w1_ref, w2_ref, w3_ref)

    def weight_copy(m, k, half):
        return pltpu.make_async_copy(
            weights[k].at[:, at(half * (D // NX) + m * SIDE, SIDE)],
            w.at[m, k, pl.ds(0, width), pl.ds(half * SIDE, SIDE)],
            wsem.at[m, k, half],
        )

    @pl.loop(0, PART)
    def _(m):
        for k in range(3):
            for half in range(NX):
                weight_copy(m, k, half).start()

    per_side = D // NX // 128
    inputs[0].wait()
    for t in range(D // 128):
        v = start_ref[:, t * 128 : (t + 1) * 128]
        xs, tl = divmod(t, per_side)
        for i in range(OWN):
            ipack[xs, i, tl : tl + 1, :] = v[i : i + 1]
            r = i * TILES + tl % TILES
            dpack[xs * NZ + tl // TILES, r : r + 1, :] = v[i : i + 1]
    for i in range(OWN):
        conv[i] = ipack[:, i].astype(BF16)
        iall[i, slot] = conv[i, xh]

    pl.semaphore_wait(barrier, len(greeted))

    for i in range(OWN):
        for k in range(1, SRC):
            to = zxpeer(k)
            push(conv.at[i, to[2]], iall.at[i, slot], snd.at[0], one.at[6 + i], to)

    inputs[1].wait()
    for k in range(STEPS):
        for t in range(D // 128):
            v = noise_ref[k, :, t * 128 : (t + 1) * 128].astype(F32)
            xs, tl = divmod(t, per_side)
            for i in range(OWN):
                r = (k + 1) * OWN * TILES + i * TILES + tl % TILES
                dpack[xs * NZ + tl // TILES, r : r + 1, :] = v[i : i + 1]
    dall[at(slot * 16, 16), :] = dpack[slot]
    for k in range(1, SRC):
        to = zxpeer(k)
        push(dpack.at[to[2] * NZ + to[0]], dall.at[at(slot * 16, 16), :], snd.at[1], one.at[1], to)

    @pl.loop(0, PART)
    def _(m):
        for k in range(3):
            w[m, k, width:PAD, :] = jnp.zeros((PAD - width, CHUNK), BF16)

    esum[...] = jnp.zeros_like(esum)
    fsend[...] = jnp.zeros_like(fsend)

    def spread(p, m):
        for rel in range(1, PEERS + 1):
            block = s_all.at[p, m, rows_y, side]
            push(block, block, snd.at[2], agx.at[p, m], xypeer(rel))

    def forward(p, m):
        arrived(s_all.at[p, m, :, pl.ds(0, SENT)], agx.at[p, m])
        term = lax.dot_general(
            w[m].reshape(3 * PAD, CHUNK), s_all[p, m], (((1,), (1,)), ((), ())), preferred_element_type=F32
        )

        @pl.when(m == 0)
        def _():
            acc[...] = term

        @pl.when(m != 0)
        def _():
            acc[...] += term

    def gathered(ref, row, stride):
        lo = ref[pl.ds(row, NZ, stride=stride), :]
        hi = ref[pl.ds(NZ * stride + row, NZ, stride=stride), :]
        return jnp.concatenate([lo, hi], axis=0)

    for i in range(OWN):
        arrived(iall.at[i, pl.ds(0, SRC - 1)], one.at[6 + i])
        wide[...] = iall[i].reshape(SRC * per_side, 128).astype(F32)
        for tl in range(per_side):
            m, pos = divmod(tl, SIDE // 128)
            lanes = at(xh * SIDE + pos * 128, 128)
            s_all[i, m, rows_y, lanes] = gathered(wide, tl, per_side).astype(BF16)
            if pos == SIDE // 128 - 1:
                spread(i, m)

    arrived(dall.at[pl.ds(0, 16 * (SRC - 1)), :], one.at[1])
    for i in range(OWN):
        for tt in range(TILES):
            state[i, :, tt * 128 : (tt + 1) * 128] = gathered(dall, i * TILES + tt, 16)

    @pl.loop(0, PART)
    def _(m):
        for k in range(3):
            for half in range(NX):
                weight_copy(m, k, half).wait()
        forward(0, m)

    def factors(p):
        h = rem(p, OWN)

        def part(q, total):
            r = q * 64
            pa, pb, pc = (acc[at(k * PAD + r, 64), :] for k in range(3))
            e = jnp.exp(-jnp.abs(pa))
            soft = jnp.maximum(pa, 0.0) + jnp.log1p(e)
            inv = 1.0 / (1.0 + e)
            sig = jnp.where(pa >= 0, inv, e * inv)
            tan = jnp.tanh(pb)
            st = soft * tan
            fac[at(r, 64), :] = (sig * tan * pc).astype(BF16)
            fac[at(PAD + r, 64), :] = (soft * (1.0 - tan * tan) * pc).astype(BF16)
            fac[at(2 * PAD + r, 64), :] = st.astype(BF16)
            return total + jnp.sum(st * pc, axis=0, keepdims=True)

        total = lax.fori_loop(0, PAD // 64, part, jnp.zeros((1, ROWS), F32))
        esum[pl.ds(h, 1), 0:ROWS] += total

    def backward(p):
        factors(p)

        @pl.loop(0, PART)
        def _(m):
            g = lax.dot_general(
                fac[...], w[m].reshape(3 * PAD, CHUNK), (((0,), (0,)), ((), ())), preferred_element_type=F32
            )
            g_all[p, m] = g.astype(BF16)
            for rel in range(1, PEERS + 1):
                to = xypeer(rel)
                block = g_all.at[p, m, at(to[1] * BLOCK, BLOCK), at(to[2] * SIDE, SIDE)]
                push(block, rx.at[p, m, rel - 1], sndg.at[p], rxs.at[p, m], to)

    def plane_sum(p, m):
        arrived(rx.at[p, m], rxs.at[p, m])
        total = g_all[p, m, rows_y, side].astype(F32)
        for k in range(PEERS):
            total = total + rx[p, m, k].astype(F32)
        zs[p, m] = total.astype(BF16)
        for jj in range(PAIR):
            j = m * PAIR + jj

            @pl.when(j == z)
            def _():
                zown[...] = total[:, jj * COLS : (jj + 1) * COLS]

            @pl.when(j != z)
            def _():
                dz = rem(j - z + NZ, NZ)
                push(
                    zs.at[p, m, :, pl.ds(jj * COLS, COLS)], zx.at[p, dz - 1], snd.at[3], zxs.at[p],
                    (j, y, xh, xl, core),
                )

    def update(p, n, h):
        arrived(zx.at[p], zxs.at[p])
        grad = zown[...]
        for k in range(NZ - 1):
            grad = grad + zx[p, k].astype(F32)
        beta = jnp.asarray(n + 1, jnp.int32).astype(F32) / STEPS
        for tt in range(TILES):
            cols = slice(tt * 128, (tt + 1) * 128)
            extra = gathered(dall, ((n + 1) * OWN + h) * TILES + tt, 16)
            old = state[h, :, cols]
            state[h, :, cols] = old - 0.05 * (old + beta * grad[:, cols]) + math.sqrt(0.1) * extra

    own_lanes = at(xh * SIDE + rem(z, PAIR) * COLS, COLS)

    def step_on(p):
        n, h = p // OWN, rem(p, OWN)
        update(p, n, h)

        @pl.when(n < STEPS - 1)
        def _():
            block = s_all.at[p + OWN, z // PAIR, rows_y, own_lanes]
            block[...] = state[h].astype(BF16)
            for dz in range(1, NZ):
                push(block, block, snd.at[4], agz.at[p, z], zpeer(dz))

    def pass_on(p, m):
        for jj in range(PAIR):
            j = m * PAIR + jj

            @pl.when(j != z)
            def _():
                arrived(s_all.at[p + OWN, m, rows_y, at(xh * SIDE + jj * COLS, COLS)], agz.at[p, j])

        spread(p + OWN, m)

    early = z < NZ // 2

    def phase(p, carry):
        backward(p)

        @pl.when(p > 0)
        def _():
            @pl.when(jnp.logical_not(early))
            def _():
                step_on(p - 1)

            @pl.loop(0, PART)
            def _(m):
                pass_on(p - 1, m)

        @pl.loop(0, PART)
        def _(m):
            plane_sum(p, m)
            forward(p + 1, m)

        @pl.when(early)
        def _():
            step_on(p)

        return carry

    lax.fori_loop(0, PHASES - 1, phase, 0)

    row = lax.broadcasted_iota(jnp.int32, (8, 128), 0)
    lane = lax.broadcasted_iota(jnp.int32, (8, 128), 1)
    own_lane = y * BLOCK + slot

    last = PHASES - 1
    backward(last)

    inputs[2].wait()
    v = esum[...] / STEPS
    for i in range(OWN):
        v = v - jnp.where((row == i) & (lane == own_lane), slw_ref[i], 0.0)
    e1[...] = v
    for rel in range(1, PEERS + 1):
        push(e1, ex.at[rel - 1], snd.at[5], one.at[3], xypeer(rel))

    @pl.when(jnp.logical_not(early))
    def _():
        update(last - 1, STEPS - 1, 0)

    @pl.loop(0, PART)
    def _(m):
        plane_sum(last, m)

    arrived(ex, one.at[3])
    total = e1[...]
    for k in range(PEERS):
        total = total + ex[k]
    e2[...] = total
    for dz in range(1, NZ):
        push(e2, ez.at[dz - 1], snd.at[6], one.at[4], zpeer(dz))

    update(last, STEPS - 1, 1)
    for i in range(OWN):
        for tt in range(TILES):
            tile = state[i, :, tt * 128 : (tt + 1) * 128]
            fsend[pl.ds(i * TILES + tt, NZ, stride=8), :] = tile[0:NZ]
            fsend[pl.ds(NZ * 8 + i * TILES + tt, NZ, stride=8), :] = tile[NZ:]
    for k in range(1, SRC):
        to = zxpeer(k)
        push(fsend.at[at((to[2] * NZ + to[0]) * 8, 8), :], fall.at[slot], snd.at[8], one.at[2], to)
    fall[slot] = fsend[at(slot * 8, 8), :]

    arrived(ez, one.at[4])
    total = e2[...]
    for k in range(NZ - 1):
        total = total + ez[k]
    e3[...] = -total
    for k in range(1, 4):
        push(e3, el.at[k - 1], snd.at[7], one.at[5], gpeer(k))
    for i in range(OWN):
        lw_ref[i] = jnp.sum(jnp.where((row == i) & (lane == own_lane), -total, 0.0))
    arrived(el, one.at[5])
    used = (row < OWN) & (lane < ROWS)
    lws = [jnp.where(used, v, -jnp.inf) for v in [-total] + [el[k] for k in range(3)]]
    top = jnp.max(jnp.maximum(jnp.maximum(lws[0], lws[1]), jnp.maximum(lws[2], lws[3])))
    mass = jnp.sum(sum(jnp.exp(v - top) for v in lws))
    lr_ref[0] = jnp.max(top + jnp.log(jnp.full((8, 128), mass, F32)) - math.log(4 * OWN * ROWS))

    arrived(fall.at[pl.ds(0, SRC - 1)], one.at[2])
    for src in range(SRC):
        for i in range(OWN):
            for tt in range(TILES):
                c = (src * TILES + tt) * 128
                out_ref[i : i + 1, c : c + 128] = fall[src, i * TILES + tt : i * TILES + tt + 1, :]

    left(iall.at[:, pl.ds(0, SRC - 1)], snd.at[0])
    left(dpack.at[pl.ds(0, SRC - 1)], snd.at[1])
    left(s_all.at[:, :, :, pl.ds(0, SENT)], snd.at[2])
    left(zx, snd.at[3])
    left(zx.at[pl.ds(0, PHASES - OWN)], snd.at[4])
    left(ex, snd.at[5])
    left(ez, snd.at[6])
    left(el, snd.at[7])
    left(fall.at[pl.ds(0, SRC - 1)], snd.at[8])
    for p in range(PHASES):
        left(g_all.at[p, :, :, pl.ds(0, SENT)], sndg.at[p])


def per_device(start_state, start_log_weight, noise, first_weight, second_weight, third_weight):
    smem = pl.BlockSpec(memory_space=pltpu.SMEM)
    hbm = pl.BlockSpec(memory_space=pl.ANY)
    tile = (8, 128)
    state, log_weight, log_ratio = pl.pallas_call(
        kernel,
        out_shape=(
            jax.ShapeDtypeStruct((OWN, D), F32),
            jax.ShapeDtypeStruct((OWN,), F32),
            jax.ShapeDtypeStruct((1,), F32),
        ),
        in_specs=[hbm] * 6,
        out_specs=(pl.BlockSpec(memory_space=pltpu.VMEM), smem, smem),
        scratch_shapes=[
            pltpu.VMEM((OWN, D), F32),
            pltpu.SMEM((OWN,), F32),
            pltpu.VMEM((STEPS, OWN, D), BF16),
            pltpu.VMEM((PART, 3, PAD, CHUNK), BF16),
            pltpu.VMEM((PHASES, PART, ROWS, CHUNK), BF16),
            pltpu.VMEM((PHASES, PART, ROWS, CHUNK), BF16),
            pltpu.VMEM((PHASES, PART, PEERS, BLOCK, SIDE), BF16),
            pltpu.VMEM((PHASES, PART, BLOCK, SIDE), BF16),
            pltpu.VMEM((PHASES, NZ - 1, BLOCK, COLS), BF16),
            pltpu.VMEM((BLOCK, COLS), F32),
            pltpu.VMEM((OWN, BLOCK, COLS), F32),
            pltpu.VMEM((3 * PAD, ROWS), F32),
            pltpu.VMEM((3 * PAD, ROWS), BF16),
            pltpu.VMEM(tile, F32),
            pltpu.VMEM((NX, OWN, 16, 128), F32),
            pltpu.VMEM((OWN, SRC, 16, 128), BF16),
            pltpu.VMEM((OWN, NX, 16, 128), BF16),
            pltpu.VMEM((SRC * 16, 128), F32),
            pltpu.VMEM((SRC, 16, 128), F32),
            pltpu.VMEM((SRC * 16, 128), F32),
            pltpu.VMEM((SRC * 8, 128), F32),
            pltpu.VMEM((SRC, 8, 128), F32),
            pltpu.VMEM(tile, F32),
            pltpu.VMEM((PEERS, *tile), F32),
            pltpu.VMEM(tile, F32),
            pltpu.VMEM((NZ - 1, *tile), F32),
            pltpu.VMEM(tile, F32),
            pltpu.VMEM((3, *tile), F32),
            pltpu.SemaphoreType.DMA((3,)),
            pltpu.SemaphoreType.DMA((PART, 3, NX)),
            pltpu.SemaphoreType.DMA((PHASES, PART)),
            pltpu.SemaphoreType.DMA((PHASES - OWN, NZ)),
            pltpu.SemaphoreType.DMA((PHASES, PART)),
            pltpu.SemaphoreType.DMA((PHASES,)),
            pltpu.SemaphoreType.DMA((8,)),
            pltpu.SemaphoreType.DMA((9,)),
            pltpu.SemaphoreType.DMA((PHASES,)),
        ],
        compiler_params=pltpu.CompilerParams(
            collective_id=0, has_side_effects=True, vmem_limit_bytes=67043328
        ),
    )(start_state, start_log_weight, noise, first_weight, second_weight, third_weight)
    return state, log_weight, log_ratio[0]


def solution(mesh):
    torus = Mesh(mesh.devices.reshape(8, 4, 2, 2, 2), AXES)
    placed = (
        P(BLK_GRP, None),
        P(BLK_GRP),
        P(None, BLK_GRP, None),
        P(BLK, None),
        P(BLK, None),
        P(BLK, None),
    )
    return jax.shard_map(
        per_device,
        mesh=torus,
        in_specs=placed,
        out_specs=(P(BLK_GRP, None), P(BLK_GRP), P()),
        check_vma=False,
    )
```

time: 456 us -> 120 us (0.26)
  blocking collectives: 206 us -> 0 us
  Pallas kernels: 0 us -> 114 us
  waiting for transfers between devices: 93 us -> 0 us
  starting transfers between devices: 42.5 us -> 0 us
  between operations: 40 us -> 2.38 us
  local copies, waits for them, and re-layouts: 30.8 us -> 2.55 us
  matrix products: 25.7 us -> 0 us
  other arithmetic: 12.5 us -> 0 us
    all_to_all x3 -> x0, blocking collectives: 138 us -> none  [the longest x2 80.3 us: sent_to_all(): return lax.all_to_all(copies, axis, split_axis=0, concat_axis=0, tiled=True)]
    pallas_call x0 -> x1, Pallas kernels: none -> 114 us  [per_device(): pl.pallas_call(kernel, out_shape=(jax.ShapeDtypeStruct((OWN, D), F32), ja...]
    all_to_all x6 -> x0, waiting for transfers between devices: 93 us -> none  [the longest x5 65.4 us: summed_on_arrival(): lax.all_to_all(parts, axis, split_axis=0, concat_axis=0, tiled=True)]
    unnamed x5 -> x0, blocking collectives: 68.3 us -> none
    all_to_all x6 -> x0, starting transfers between devices: 42.5 us -> none  [the longest x5 36.4 us: summed_on_arrival(): lax.all_to_all(parts, axis, split_axis=0, concat_axis=0, tiled=True)]
    dot_general x18 -> x0, matrix products: 25.7 us -> none  [the longest x9 15 us: back_product(): term = jnp.dot(factor, weight, preferred_element_type=jnp.float32)]
    reshape x6 -> x0, local copies, waits for them, and re-layouts: 14.9 us -> none  [the longest x3 10.5 us: split_up(): return jnp.moveaxis(array.reshape(*before, devices, -1, *after), dim, 0)]
    reduce_sum x7 -> x0, other arithmetic: 8.17 us -> none  [the longest x6 6.93 us: summed_on_arrival(): return arrived.sum(axis=0)]
  transfers between devices with their start and end apart: 6 -> 0, of which waited for: 5 -> 0; matrix products, arithmetic and copies ran while one was open for 6% -> 0% of each run, Pallas kernels for 0% -> 0%
where the time goes in v2:
time: 120 us; the launch traced here: 119 us
  Pallas kernels  114 us (95%)
  local copies, waits for them, and re-layouts  2.55 us (2%)
  between operations  2.38 us (2%)
    pallas_call x1, Pallas kernels, per_device(): pl.pallas_call(kernel, out_shape=(jax.ShapeDtypeStruct((OWN, D), F32), ja...  114 us
    unnamed x2, local copies, waits for them, and re-layouts  2.55 us

profile of v2, /device:TPU:32, one launch (start us, length us, event | category | flops | bytes accessed | tf_op | source)
XLA Modules:
  0.0 119.4 jit_solution(6184213747856993824)
XLA Ops:
  0.6 114.4 %shard_map.85 = (f32[2,4096]{1,0:T(2,128)}, f32[2]{0:T(128)}, f32[1]{0:T(128)}) custom-call(f32[2,4096]{1,0:T(2,128)} %start_hbm.1, f32[2]{0:T(128)} %slw_hbm.1, bf16[3,2,4096]{2,1,0:T(2,128)(2,1)} %noise_hbm.1, bf16[224,4096]{1,0:T(8,128)(2,1)} %w1_ref.1, bf16[224,4096]{1,0:T(8,128)(2,1)} %w2_ref.1, bf16[224,4096]{1,0:T(8,128)(2,1)} %w3_ref.1), custom_call_target="tpu_custom_call" | custom-call | tf_op jit(solution)/shard_map/pallas_call | solution.py:410
  115.1 1.4 %copy.12 = f32[2,4096]{1,0:T(2,128)} copy(f32[2,4096]{1,0:T(2,128)} %get-tuple-element.12) | data formatting | bytes 65536
  116.4 1.2 copy.13

commit v3 on v2

--- a/solution.py
+++ b/solution.py
@@ -47,8 +47,8 @@
     out_ref, lw_ref, lr_ref,
     start_ref, slw_ref, noise_ref,
     w, s_all, g_all, rx, zs, zx, zown, state, acc, fac, esum,
-    ipack, iall, conv, wide, dpack, dall, fsend, fall, e1, ex, e2, ez, e3, el,
-    insem, wsem, agx, agz, rxs, zxs, one, snd, sndg,
+    ipack, iall, conv, wide, dpack, dall, fsend, fall, hsend, hall, e1, ex, e2, ez, e3, el,
+    insem, wsem, agx, agz, rxs, zxs, hsem, one, snd, sndg,
 ):
     z, y, xh, xl, core = (lax.axis_index(name) for name in AXES)
     width = w1_ref.shape[0]
@@ -227,10 +227,8 @@
         total = lax.fori_loop(0, PAD // 64, part, jnp.zeros((1, ROWS), F32))
         esum[pl.ds(h, 1), 0:ROWS] += total
 
-    def backward(p):
-        factors(p)
-
-        @pl.loop(0, PART)
+    def backward(p, first, end):
+        @pl.loop(first, end)
         def _(m):
             g = lax.dot_general(
                 fac[...], w[m].reshape(3 * PAD, CHUNK), (((0,), (0,)), ((), ())), preferred_element_type=F32
@@ -241,11 +239,15 @@
                 block = g_all.at[p, m, at(to[1] * BLOCK, BLOCK), at(to[2] * SIDE, SIDE)]
                 push(block, rx.at[p, m, rel - 1], sndg.at[p], rxs.at[p, m], to)
 
-    def plane_sum(p, m):
+    def plane_total(p, m):
         arrived(rx.at[p, m], rxs.at[p, m])
         total = g_all[p, m, rows_y, side].astype(F32)
         for k in range(PEERS):
             total = total + rx[p, m, k].astype(F32)
+        return total
+
+    def plane_sum(p, m):
+        total = plane_total(p, m)
         zs[p, m] = total.astype(BF16)
         for jj in range(PAIR):
             j = m * PAIR + jj
@@ -279,13 +281,25 @@
     def step_on(p):
         n, h = p // OWN, rem(p, OWN)
         update(p, n, h)
-
-        @pl.when(n < STEPS - 1)
+        block = s_all.at[p + OWN, z // PAIR, rows_y, own_lanes]
+        block[...] = state[h].astype(BF16)
+        for dz in range(1, NZ):
+            push(block, block, snd.at[4], agz.at[p, z], zpeer(dz))
+
+        @pl.when(n == STEPS - 2)
         def _():
-            block = s_all.at[p + OWN, z // PAIR, rows_y, own_lanes]
-            block[...] = state[h].astype(BF16)
-            for dz in range(1, NZ):
-                push(block, block, snd.at[4], agz.at[p, z], zpeer(dz))
+            base = h * SRC * 8
+            for tt in range(TILES):
+                tile = state[h, :, tt * 128 : (tt + 1) * 128]
+                fsend[pl.ds(base + tt, NZ, stride=8), :] = tile[0:NZ]
+                fsend[pl.ds(base + NZ * 8 + tt, NZ, stride=8), :] = tile[NZ:]
+            for k in range(1, SRC):
+                to = zxpeer(k)
+                push(
+                    fsend.at[at(base + (to[2] * NZ + to[0]) * 8, 8), :], fall.at[h, slot],
+                    snd.at[8], one.at[2], to,
+                )
+            fall[h, slot] = fsend[at(base + slot * 8, 8), :]
 
     def pass_on(p, m):
         for jj in range(PAIR):
@@ -299,15 +313,20 @@
 
     early = z < NZ // 2
 
+    half = PART // 2
+
     def phase(p, carry):
-        backward(p)
+        factors(p)
+        backward(p, 0, half)
+
+        @pl.when((p > 0) & jnp.logical_not(early))
+        def _():
+            step_on(p - 1)
+
+        backward(p, half, PART)
 
         @pl.when(p > 0)
         def _():
-            @pl.when(jnp.logical_not(early))
-            def _():
-                step_on(p - 1)
-
             @pl.loop(0, PART)
             def _(m):
                 pass_on(p - 1, m)
@@ -315,6 +334,9 @@
         @pl.loop(0, PART)
         def _(m):
             plane_sum(p, m)
+
+        @pl.loop(0, PART)
+        def _(m):
             forward(p + 1, m)
 
         @pl.when(early)
@@ -323,14 +345,77 @@
 
         return carry
 
-    lax.fori_loop(0, PHASES - 1, phase, 0)
+    lax.fori_loop(0, PHASES - OWN, phase, 0)
+
+    def home_sum(h, pair):
+        base = (h * 2 + pair) * SRC * 8
+
+        @pl.loop(0, PART // 2)
+        def _(q):
+            total = plane_total(PHASES - OWN + h, pair * (PART // 2) + q)
+            for pos in range(SIDE // 128):
+                tile = total[:, pos * 128 : (pos + 1) * 128]
+                r = base + q * (SIDE // 128) + pos
+                hsend[pl.ds(r, NZ, stride=8), :] = tile[0:NZ]
+                hsend[pl.ds(r + NZ * 8, NZ, stride=8), :] = tile[NZ:]
+
+        for k in range(1, SRC):
+            to = zxpeer(k)
+            push(
+                hsend.at[at(base + (to[2] * NZ + to[0]) * 8, 8), :], hall.at[h, pair, slot],
+                snd.at[9], hsem.at[h], to,
+            )
+        hall[h, pair, slot] = hsend[at(base + slot * 8, 8), :]
+
+    def home_base():
+        arrived(fall.at[:, pl.ds(0, SRC - 1)], one.at[2])
+        for src in range(SRC):
+            for tt in range(TILES):
+                c = (src * TILES + tt) * 128
+                extra = noise_ref[STEPS - 1, :, c : c + 128].astype(F32)
+                for i in range(OWN):
+                    old = fall[i, src, tt : tt + 1, :]
+                    out_ref[i : i + 1, c : c + 128] = old - 0.05 * old + math.sqrt(0.1) * extra[i : i + 1]
+
+    def home_end(h):
+        arrived(hall.at[h, :, pl.ds(0, SRC - 1)], hsem.at[h])
+        for xs in range(NX):
+            for pair in range(2):
+                grad = hall[h, pair, xs * NZ]
+                for k in range(1, NZ):
+                    grad = grad + hall[h, pair, xs * NZ + k]
+                grad = 0.05 * grad
+                for r in range(8):
+                    c = (xs * per_side + pair * 8 + r) * 128
+                    out_ref[h : h + 1, c : c + 128] -= grad[r : r + 1]
+
+    p = PHASES - OWN
+    factors(p)
+    backward(p, 0, half)
+
+    @pl.when(jnp.logical_not(early))
+    def _():
+        step_on(p - 1)
+
+    backward(p, half, PART)
+
+    @pl.loop(0, PART)
+    def _(m):
+        pass_on(p - 1, m)
+
+    home_sum(0, 0)
+    home_sum(0, 1)
+
+    @pl.loop(0, PART)
+    def _(m):
+        forward(p + 1, m)
 
     row = lax.broadcasted_iota(jnp.int32, (8, 128), 0)
     lane = lax.broadcasted_iota(jnp.int32, (8, 128), 1)
     own_lane = y * BLOCK + slot
 
-    last = PHASES - 1
-    backward(last)
+    factors(p + 1)
+    backward(p + 1, 0, PART)
 
     inputs[2].wait()
     v = esum[...] / STEPS
@@ -340,13 +425,9 @@
     for rel in range(1, PEERS + 1):
         push(e1, ex.at[rel - 1], snd.at[5], one.at[3], xypeer(rel))
 
-    @pl.when(jnp.logical_not(early))
-    def _():
-        update(last - 1, STEPS - 1, 0)
-
-    @pl.loop(0, PART)
-    def _(m):
-        plane_sum(last, m)
+    home_base()
+    home_end(0)
+    home_sum(1, 0)
 
     arrived(ex, one.at[3])
     total = e1[...]
@@ -356,16 +437,7 @@
     for dz in range(1, NZ):
         push(e2, ez.at[dz - 1], snd.at[6], one.at[4], zpeer(dz))
 
-    update(last, STEPS - 1, 1)
-    for i in range(OWN):
-        for tt in range(TILES):
-            tile = state[i, :, tt * 128 : (tt + 1) * 128]
-            fsend[pl.ds(i * TILES + tt, NZ, stride=8), :] = tile[0:NZ]
-            fsend[pl.ds(NZ * 8 + i * TILES + tt, NZ, stride=8), :] = tile[NZ:]
-    for k in range(1, SRC):
-        to = zxpeer(k)
-        push(fsend.at[at((to[2] * NZ + to[0]) * 8, 8), :], fall.at[slot], snd.at[8], one.at[2], to)
-    fall[slot] = fsend[at(slot * 8, 8), :]
+    home_sum(1, 1)
 
     arrived(ez, one.at[4])
     total = e2[...]
@@ -383,22 +455,18 @@
     mass = jnp.sum(sum(jnp.exp(v - top) for v in lws))
     lr_ref[0] = jnp.max(top + jnp.log(jnp.full((8, 128), mass, F32)) - math.log(4 * OWN * ROWS))
 
-    arrived(fall.at[pl.ds(0, SRC - 1)], one.at[2])
-    for src in range(SRC):
-        for i in range(OWN):
-            for tt in range(TILES):
-                c = (src * TILES + tt) * 128
-                out_ref[i : i + 1, c : c + 128] = fall[src, i * TILES + tt : i * TILES + tt + 1, :]
+    home_end(1)
 
     left(iall.at[:, pl.ds(0, SRC - 1)], snd.at[0])
     left(dpack.at[pl.ds(0, SRC - 1)], snd.at[1])
     left(s_all.at[:, :, :, pl.ds(0, SENT)], snd.at[2])
     left(zx, snd.at[3])
-    left(zx.at[pl.ds(0, PHASES - OWN)], snd.at[4])
+    left(zx, snd.at[4])
     left(ex, snd.at[5])
     left(ez, snd.at[6])
     left(el, snd.at[7])
-    left(fall.at[pl.ds(0, SRC - 1)], snd.at[8])
+    left(fall.at[:, pl.ds(0, SRC - 1)], snd.at[8])
+    left(hall.at[:, :, pl.ds(0, SRC - 1)], snd.at[9])
     for p in range(PHASES):
         left(g_all.at[p, :, :, pl.ds(0, SENT)], sndg.at[p])
 
@@ -424,8 +492,8 @@
             pltpu.VMEM((PHASES, PART, ROWS, CHUNK), BF16),
             pltpu.VMEM((PHASES, PART, ROWS, CHUNK), BF16),
             pltpu.VMEM((PHASES, PART, PEERS, BLOCK, SIDE), BF16),
-            pltpu.VMEM((PHASES, PART, BLOCK, SIDE), BF16),
-            pltpu.VMEM((PHASES, NZ - 1, BLOCK, COLS), BF16),
+            pltpu.VMEM((PHASES - OWN, PART, BLOCK, SIDE), BF16),
+            pltpu.VMEM((PHASES - OWN, NZ - 1, BLOCK, COLS), BF16),
             pltpu.VMEM((BLOCK, COLS), F32),
             pltpu.VMEM((OWN, BLOCK, COLS), F32),
             pltpu.VMEM((3 * PAD, ROWS), F32),
@@ -437,8 +505,10 @@
             pltpu.VMEM((SRC * 16, 128), F32),
             pltpu.VMEM((SRC, 16, 128), F32),
             pltpu.VMEM((SRC * 16, 128), F32),
-            pltpu.VMEM((SRC * 8, 128), F32),
-            pltpu.VMEM((SRC, 8, 128), F32),
+            pltpu.VMEM((OWN * SRC * 8, 128), F32),
+            pltpu.VMEM((OWN, SRC, 8, 128), F32),
+            pltpu.VMEM((OWN * 2 * SRC * 8, 128), F32),
+            pltpu.VMEM((OWN, 2, SRC, 8, 128), F32),
             pltpu.VMEM(tile, F32),
             pltpu.VMEM((PEERS, *tile), F32),
             pltpu.VMEM(tile, F32),
@@ -450,9 +520,10 @@
             pltpu.SemaphoreType.DMA((PHASES, PART)),
             pltpu.SemaphoreType.DMA((PHASES - OWN, NZ)),
             pltpu.SemaphoreType.DMA((PHASES, PART)),
-            pltpu.SemaphoreType.DMA((PHASES,)),
+            pltpu.SemaphoreType.DMA((PHASES - OWN,)),
+            pltpu.SemaphoreType.DMA((OWN,)),
             pltpu.SemaphoreType.DMA((8,)),
-            pltpu.SemaphoreType.DMA((9,)),
+            pltpu.SemaphoreType.DMA((10,)),
             pltpu.SemaphoreType.DMA((PHASES,)),
         ],
         compiler_params=pltpu.CompilerParams(

time: 120 us -> 119 us (level); the launches traced: 119 us -> 116 us
  Pallas kernels: 114 us -> 112 us
    pallas_call x1, Pallas kernels: 114 us -> 112 us  [per_device(): pl.pallas_call(kernel, out_shape=(jax.ShapeDtypeStruct((OWN, D), F32), ja...]
where the time goes in v3:
time: 119 us; the launch traced here: 116 us
  Pallas kernels  112 us (94%)
  local copies, waits for them, and re-layouts  2.55 us (2%)
  between operations  2.38 us (2%)
    pallas_call x1, Pallas kernels, per_device(): pl.pallas_call(kernel, out_shape=(jax.ShapeDtypeStruct((OWN, D), F32), ja...  112 us
    unnamed x2, local copies, waits for them, and re-layouts  2.55 us

profile of v3, /device:TPU:32, one launch (start us, length us, event | category | flops | bytes accessed | tf_op | source)
XLA Modules:
  0.0 116.4 jit_solution(13238465530042480677)
XLA Ops:
  0.6 111.5 %shard_map.85 = (f32[2,4096]{1,0:T(2,128)}, f32[2]{0:T(128)}, f32[1]{0:T(128)}) custom-call(f32[2,4096]{1,0:T(2,128)} %start_hbm.1, f32[2]{0:T(128)} %slw_hbm.1, bf16[3,2,4096]{2,1,0:T(2,128)(2,1)} %noise_hbm.1, bf16[224,4096]{1,0:T(8,128)(2,1)} %w1_ref.1, bf16[224,4096]{1,0:T(8,128)(2,1)} %w2_ref.1, bf16[224,4096]{1,0:T(8,128)(2,1)} %w3_ref.1), custom_call_target="tpu_custom_call" | custom-call | tf_op jit(solution)/shard_map/pallas_call | solution.py:478
  112.2 1.4 %copy.12 = f32[2,4096]{1,0:T(2,128)} copy(f32[2,4096]{1,0:T(2,128)} %get-tuple-element.12) | data formatting | bytes 65536
  113.5 1.2 %copy.13 = f32[2]{0:T(128)} copy(f32[2]{0:T(128)} %get-tuple-element.13) | data formatting | bytes 16

commit v4 on v2

--- a/solution.py
+++ b/solution.py
@@ -32,6 +32,11 @@
 PAD = 256
 PEERS = NY * NX - 1
 SENT = CHUNK * PEERS // (PEERS + 1)
+FAR_XY = (5, 4, 3, 7, 2, 6, 1)
+FAR_Z = (4, 3, 5, 2, 6, 1, 7)
+FAR_ZX = tuple(NX * dz + 1 for dz in FAR_Z[:3]) + tuple(NX * dz for dz in FAR_Z[:3]) + tuple(
+    NX * dz + dx for dz in FAR_Z[3:] for dx in (1, 0)
+) + (1,)
 
 
 def rem(a, n):
@@ -136,7 +141,7 @@
     pl.semaphore_wait(barrier, len(greeted))
 
     for i in range(OWN):
-        for k in range(1, SRC):
+        for k in FAR_ZX:
             to = zxpeer(k)
             push(conv.at[i, to[2]], iall.at[i, slot], snd.at[0], one.at[6 + i], to)
 
@@ -149,7 +154,7 @@
                 r = (k + 1) * OWN * TILES + i * TILES + tl % TILES
                 dpack[xs * NZ + tl // TILES, r : r + 1, :] = v[i : i + 1]
     dall[at(slot * 16, 16), :] = dpack[slot]
-    for k in range(1, SRC):
+    for k in FAR_ZX:
         to = zxpeer(k)
         push(dpack.at[to[2] * NZ + to[0]], dall.at[at(slot * 16, 16), :], snd.at[1], one.at[1], to)
 
@@ -162,7 +167,7 @@
     fsend[...] = jnp.zeros_like(fsend)
 
     def spread(p, m):
-        for rel in range(1, PEERS + 1):
+        for rel in FAR_XY:
             block = s_all.at[p, m, rows_y, side]
             push(block, block, snd.at[2], agx.at[p, m], xypeer(rel))
 
@@ -236,7 +241,7 @@
                 fac[...], w[m].reshape(3 * PAD, CHUNK), (((0,), (0,)), ((), ())), preferred_element_type=F32
             )
             g_all[p, m] = g.astype(BF16)
-            for rel in range(1, PEERS + 1):
+            for rel in FAR_XY:
                 to = xypeer(rel)
                 block = g_all.at[p, m, at(to[1] * BLOCK, BLOCK), at(to[2] * SIDE, SIDE)]
                 push(block, rx.at[p, m, rel - 1], sndg.at[p], rxs.at[p, m], to)
@@ -284,7 +289,7 @@
         def _():
             block = s_all.at[p + OWN, z // PAIR, rows_y, own_lanes]
             block[...] = state[h].astype(BF16)
-            for dz in range(1, NZ):
+            for dz in FAR_Z:
                 push(block, block, snd.at[4], agz.at[p, z], zpeer(dz))
 
     def pass_on(p, m):
@@ -315,6 +320,9 @@
         @pl.loop(0, PART)
         def _(m):
             plane_sum(p, m)
+
+        @pl.loop(0, PART)
+        def _(m):
             forward(p + 1, m)
 
         @pl.when(early)
@@ -362,7 +370,7 @@
             tile = state[i, :, tt * 128 : (tt + 1) * 128]
             fsend[pl.ds(i * TILES + tt, NZ, stride=8), :] = tile[0:NZ]
             fsend[pl.ds(NZ * 8 + i * TILES + tt, NZ, stride=8), :] = tile[NZ:]
-    for k in range(1, SRC):
+    for k in FAR_ZX:
         to = zxpeer(k)
         push(fsend.at[at((to[2] * NZ + to[0]) * 8, 8), :], fall.at[slot], snd.at[8], one.at[2], to)
     fall[slot] = fsend[at(slot * 8, 8), :]

time: 120 us -> 114 us (0.950)
  Pallas kernels: 114 us -> 109 us
    pallas_call x1, Pallas kernels: 114 us -> 109 us  [per_device(): pl.pallas_call(kernel, out_shape=(jax.ShapeDtypeStruct((OWN, D), F32), ja...]
where the time goes in v4:
time: 114 us
  Pallas kernels  109 us (96%)
  local copies, waits for them, and re-layouts  2.55 us (2%)
  between operations  2.38 us (2%)
    pallas_call x1, Pallas kernels, per_device(): pl.pallas_call(kernel, out_shape=(jax.ShapeDtypeStruct((OWN, D), F32), ja...  109 us
    unnamed x2, local copies, waits for them, and re-layouts  2.55 us

profile of v4, /device:TPU:32, one launch (start us, length us, event | category | flops | bytes accessed | tf_op | source)
XLA Modules:
  0.0 114.0 jit_solution(4013099799976836338)
XLA Ops:
  0.6 109.1 %shard_map.85 = (f32[2,4096]{1,0:T(2,128)}, f32[2]{0:T(128)}, f32[1]{0:T(128)}) custom-call(f32[2,4096]{1,0:T(2,128)} %start_hbm.1, f32[2]{0:T(128)} %slw_hbm.1, bf16[3,2,4096]{2,1,0:T(2,128)(2,1)} %noise_hbm.1, bf16[224,4096]{1,0:T(8,128)(2,1)} %w1_ref.1, bf16[224,4096]{1,0:T(8,128)(2,1)} %w2_ref.1, bf16[224,4096]{1,0:T(8,128)(2,1)} %w3_ref.1), custom_call_target="tpu_custom_call" | custom-call | tf_op jit(solution)/shard_map/pallas_call | solution.py:418
  109.7 1.4 %copy.12 = f32[2,4096]{1,0:T(2,128)} copy(f32[2,4096]{1,0:T(2,128)} %get-tuple-element.12) | data formatting | bytes 65536
  111.1 1.2 %copy.13 = f32[2]{0:T(128)} copy(f32[2]{0:T(128)} %get-tuple-element.13) | data formatting | bytes 16

commit v5 on v4

--- a/solution.py
+++ b/solution.py
@@ -257,7 +257,7 @@
 
             @pl.when(j == z)
             def _():
-                zown[...] = total[:, jj * COLS : (jj + 1) * COLS]
+                zown[rem(p, OWN)] = total[:, jj * COLS : (jj + 1) * COLS]
 
             @pl.when(j != z)
             def _():
@@ -269,7 +269,7 @@
 
     def update(p, n, h):
         arrived(zx.at[p], zxs.at[p])
-        grad = zown[...]
+        grad = zown[h]
         for k in range(NZ - 1):
             grad = grad + zx[p, k].astype(F32)
         beta = jnp.asarray(n + 1, jnp.int32).astype(F32) / STEPS
@@ -285,12 +285,10 @@
         n, h = p // OWN, rem(p, OWN)
         update(p, n, h)
 
-        @pl.when(n < STEPS - 1)
-        def _():
-            block = s_all.at[p + OWN, z // PAIR, rows_y, own_lanes]
-            block[...] = state[h].astype(BF16)
-            for dz in FAR_Z:
-                push(block, block, snd.at[4], agz.at[p, z], zpeer(dz))
+        block = s_all.at[p + OWN, z // PAIR, rows_y, own_lanes]
+        block[...] = state[h].astype(BF16)
+        for dz in FAR_Z:
+            push(block, block, snd.at[4], agz.at[p, z], zpeer(dz))
 
     def pass_on(p, m):
         for jj in range(PAIR):
@@ -302,42 +300,34 @@
 
         spread(p + OWN, m)
 
-    early = z < NZ // 2
-
-    def phase(p, carry):
-        backward(p)
-
-        @pl.when(p > 0)
-        def _():
-            @pl.when(jnp.logical_not(early))
-            def _():
-                step_on(p - 1)
-
-            @pl.loop(0, PART)
-            def _(m):
-                pass_on(p - 1, m)
-
+    def each(part, *args):
         @pl.loop(0, PART)
         def _(m):
-            plane_sum(p, m)
-
-        @pl.loop(0, PART)
-        def _(m):
-            forward(p + 1, m)
-
-        @pl.when(early)
-        def _():
-            step_on(p)
-
+            part(*args, m)
+
+    def step(n, carry):
+        first, second = n * OWN, n * OWN + 1
+        backward(first)
+        each(forward, second)
+        backward(second)
+        each(plane_sum, first)
+        each(plane_sum, second)
+        step_on(first)
+        step_on(second)
+        each(pass_on, first)
+        each(pass_on, second)
+        each(forward, first + OWN)
         return carry
 
-    lax.fori_loop(0, PHASES - 1, phase, 0)
+    lax.fori_loop(0, STEPS - 1, step, 0)
 
     row = lax.broadcasted_iota(jnp.int32, (8, 128), 0)
     lane = lax.broadcasted_iota(jnp.int32, (8, 128), 1)
     own_lane = y * BLOCK + slot
 
     last = PHASES - 1
+    backward(last - 1)
+    each(forward, last)
     backward(last)
 
     inputs[2].wait()
@@ -348,14 +338,7 @@
     for rel in range(1, PEERS + 1):
         push(e1, ex.at[rel - 1], snd.at[5], one.at[3], xypeer(rel))
 
-    @pl.when(jnp.logical_not(early))
-    def _():
-        update(last - 1, STEPS - 1, 0)
-
-    @pl.loop(0, PART)
-    def _(m):
-        plane_sum(last, m)
-
+    each(plane_sum, last - 1)
     arrived(ex, one.at[3])
     total = e1[...]
     for k in range(PEERS):
@@ -364,6 +347,8 @@
     for dz in range(1, NZ):
         push(e2, ez.at[dz - 1], snd.at[6], one.at[4], zpeer(dz))
 
+    each(plane_sum, last)
+    update(last - 1, STEPS - 1, 0)
     update(last, STEPS - 1, 1)
     for i in range(OWN):
         for tt in range(TILES):
@@ -434,7 +419,7 @@
             pltpu.VMEM((PHASES, PART, PEERS, BLOCK, SIDE), BF16),
             pltpu.VMEM((PHASES, PART, BLOCK, SIDE), BF16),
             pltpu.VMEM((PHASES, NZ - 1, BLOCK, COLS), BF16),
-            pltpu.VMEM((BLOCK, COLS), F32),
+            pltpu.VMEM((OWN, BLOCK, COLS), F32),
             pltpu.VMEM((OWN, BLOCK, COLS), F32),
             pltpu.VMEM((3 * PAD, ROWS), F32),
             pltpu.VMEM((3 * PAD, ROWS), BF16),

time: 114 us -> 112 us (0.982)
  Pallas kernels: 109 us -> 107 us
    pallas_call x1, Pallas kernels: 109 us -> 107 us  [per_device(): pl.pallas_call(kernel, out_shape=(jax.ShapeDtypeStruct((OWN, D), F32), ja...]
where the time goes in v5:
time: 112 us
  Pallas kernels  107 us (96%)
  local copies, waits for them, and re-layouts  2.55 us (2%)
  between operations  2.38 us (2%)
    pallas_call x1, Pallas kernels, per_device(): pl.pallas_call(kernel, out_shape=(jax.ShapeDtypeStruct((OWN, D), F32), ja...  107 us
    unnamed x2, local copies, waits for them, and re-layouts  2.55 us

profile of v5, /device:TPU:32, one launch (start us, length us, event | category | flops | bytes accessed | tf_op | source)
XLA Modules:
  0.0 111.7 jit_solution(850088144670849047)
XLA Ops:
  0.6 106.8 %shard_map.85 = (f32[2,4096]{1,0:T(2,128)}, f32[2]{0:T(128)}, f32[1]{0:T(128)}) custom-call(f32[2,4096]{1,0:T(2,128)} %start_hbm.1, f32[2]{0:T(128)} %slw_hbm.1, bf16[3,2,4096]{2,1,0:T(2,128)(2,1)} %noise_hbm.1, bf16[224,4096]{1,0:T(8,128)(2,1)} %w1_ref.1, bf16[224,4096]{1,0:T(8,128)(2,1)} %w2_ref.1, bf16[224,4096]{1,0:T(8,128)(2,1)} %w3_ref.1), custom_call_target="tpu_custom_call" | custom-call | tf_op jit(solution)/shard_map/pallas_call | solution.py:403
  107.4 1.4 %copy.12 = f32[2,4096]{1,0:T(2,128)} copy(f32[2,4096]{1,0:T(2,128)} %get-tuple-element.12) | data formatting | bytes 65536
  108.8 1.2 %copy.13 = f32[2]{0:T(128)} copy(f32[2]{0:T(128)} %get-tuple-element.13) | data formatting | bytes 16

commit v6 on v5

--- a/solution.py
+++ b/solution.py
@@ -171,17 +171,17 @@
             block = s_all.at[p, m, rows_y, side]
             push(block, block, snd.at[2], agx.at[p, m], xypeer(rel))
 
-    def forward(p, m):
+    def forward(p, m, start):
         arrived(s_all.at[p, m, :, pl.ds(0, SENT)], agx.at[p, m])
         term = lax.dot_general(
             w[m].reshape(3 * PAD, CHUNK), s_all[p, m], (((1,), (1,)), ((), ())), preferred_element_type=F32
         )
 
-        @pl.when(m == 0)
+        @pl.when(start)
         def _():
             acc[...] = term
 
-        @pl.when(m != 0)
+        @pl.when(jnp.logical_not(start))
         def _():
             acc[...] += term
 
@@ -210,7 +210,7 @@
         for k in range(3):
             for half in range(NX):
                 weight_copy(m, k, half).wait()
-        forward(0, m)
+        forward(0, m, m == 0)
 
     def factors(p):
         h = rem(p, OWN)
@@ -279,26 +279,36 @@
             old = state[h, :, cols]
             state[h, :, cols] = old - 0.05 * (old + beta * grad[:, cols]) + math.sqrt(0.1) * extra
 
-    own_lanes = at(xh * SIDE + rem(z, PAIR) * COLS, COLS)
+    def owned(p, j):
+        return s_all.at[p, j // PAIR, rows_y, at(xh * SIDE + rem(j, PAIR) * COLS, COLS)]
+
+    def spread_owned(p, j):
+        for rel in FAR_XY:
+            push(owned(p, j), owned(p, j), snd.at[2], agx.at[p, j // PAIR], xypeer(rel))
 
     def step_on(p):
         n, h = p // OWN, rem(p, OWN)
         update(p, n, h)
 
-        block = s_all.at[p + OWN, z // PAIR, rows_y, own_lanes]
+        block = owned(p + OWN, z)
         block[...] = state[h].astype(BF16)
         for dz in FAR_Z:
             push(block, block, snd.at[4], agz.at[p, z], zpeer(dz))
-
-    def pass_on(p, m):
-        for jj in range(PAIR):
-            j = m * PAIR + jj
-
-            @pl.when(j != z)
-            def _():
-                arrived(s_all.at[p + OWN, m, rows_y, at(xh * SIDE + jj * COLS, COLS)], agz.at[p, j])
-
-        spread(p + OWN, m)
+        spread_owned(p + OWN, z)
+
+    def pass_on(p):
+        @pl.loop(0, NZ - 1)
+        def _(i):
+            k = i // 2 + 1
+            j = rem(z + jnp.where(rem(i, 2) == 0, k, NZ - k), NZ)
+            arrived(owned(p + OWN, j), agz.at[p, j])
+            spread_owned(p + OWN, j)
+
+    def forwards(p):
+        @pl.loop(0, PART)
+        def _(k):
+            turn = jnp.where(k == 2, 3, jnp.where(k == 3, 2, k))
+            forward(p, rem(z // PAIR + turn, PART), k == 0)
 
     def each(part, *args):
         @pl.loop(0, PART)
@@ -308,15 +318,15 @@
     def step(n, carry):
         first, second = n * OWN, n * OWN + 1
         backward(first)
-        each(forward, second)
+        forwards(second)
         backward(second)
         each(plane_sum, first)
         each(plane_sum, second)
         step_on(first)
         step_on(second)
-        each(pass_on, first)
-        each(pass_on, second)
-        each(forward, first + OWN)
+        pass_on(first)
+        pass_on(second)
+        forwards(first + OWN)
         return carry
 
     lax.fori_loop(0, STEPS - 1, step, 0)
@@ -327,7 +337,7 @@
 
     last = PHASES - 1
     backward(last - 1)
-    each(forward, last)
+    forwards(last)
     backward(last)
 
     inputs[2].wait()

time: 112 us -> 110 us (0.982)
  Pallas kernels: 107 us -> 105 us
    pallas_call x1, Pallas kernels: 107 us -> 105 us  [per_device(): pl.pallas_call(kernel, out_shape=(jax.ShapeDtypeStruct((OWN, D), F32), ja...]
where the time goes in v6:
time: 110 us
  Pallas kernels  105 us (95%)
  local copies, waits for them, and re-layouts  2.55 us (2%)
  between operations  2.38 us (2%)
    pallas_call x1, Pallas kernels, per_device(): pl.pallas_call(kernel, out_shape=(jax.ShapeDtypeStruct((OWN, D), F32), ja...  105 us
    unnamed x2, local copies, waits for them, and re-layouts  2.55 us

profile of v6, /device:TPU:32, one launch (start us, length us, event | category | flops | bytes accessed | tf_op | source)
XLA Modules:
  0.0 110.1 jit_solution(7383247529376865688)
XLA Ops:
  0.6 105.2 %shard_map.85 = (f32[2,4096]{1,0:T(2,128)}, f32[2]{0:T(128)}, f32[1]{0:T(128)}) custom-call(f32[2,4096]{1,0:T(2,128)} %start_hbm.1, f32[2]{0:T(128)} %slw_hbm.1, bf16[3,2,4096]{2,1,0:T(2,128)(2,1)} %noise_hbm.1, bf16[224,4096]{1,0:T(8,128)(2,1)} %w1_ref.1, bf16[224,4096]{1,0:T(8,128)(2,1)} %w2_ref.1, bf16[224,4096]{1,0:T(8,128)(2,1)} %w3_ref.1), custom_call_target="tpu_custom_call" | custom-call | tf_op jit(solution)/shard_map/pallas_call | solution.py:413
  105.9 1.4 %copy.12 = f32[2,4096]{1,0:T(2,128)} copy(f32[2,4096]{1,0:T(2,128)} %get-tuple-element.12) | data formatting | bytes 65536
  107.2 1.2 %copy.13 = f32[2]{0:T(128)} copy(f32[2]{0:T(128)} %get-tuple-element.13) | data formatting | bytes 16

commit v7 on v6

--- a/solution.py
+++ b/solution.py
@@ -321,8 +321,12 @@
         forwards(second)
         backward(second)
         each(plane_sum, first)
-        each(plane_sum, second)
+        @pl.loop(0, PART - 1)
+        def _(m):
+            plane_sum(second, m)
+
         step_on(first)
+        plane_sum(second, PART - 1)
         step_on(second)
         pass_on(first)
         pass_on(second)

time: 110 us -> 111 us (level); the launches traced: 110 us -> 110 us
  no operation moved by 1% of the time
where the time goes in v7:
time: 111 us; the launch traced here: 110 us
  Pallas kernels  105 us (95%)
  local copies, waits for them, and re-layouts  2.55 us (2%)
  between operations  2.38 us (2%)
    pallas_call x1, Pallas kernels, per_device(): pl.pallas_call(kernel, out_shape=(jax.ShapeDtypeStruct((OWN, D), F32), ja...  105 us
    unnamed x2, local copies, waits for them, and re-layouts  2.55 us

profile of v7, /device:TPU:32, one launch (start us, length us, event | category | flops | bytes accessed | tf_op | source)
XLA Modules:
  0.0 109.9 jit_solution(15290710221025303693)
XLA Ops:
  0.6 105.0 %shard_map.85 = (f32[2,4096]{1,0:T(2,128)}, f32[2]{0:T(128)}, f32[1]{0:T(128)}) custom-call(f32[2,4096]{1,0:T(2,128)} %start_hbm.1, f32[2]{0:T(128)} %slw_hbm.1, bf16[3,2,4096]{2,1,0:T(2,128)(2,1)} %noise_hbm.1, bf16[224,4096]{1,0:T(8,128)(2,1)} %w1_ref.1, bf16[224,4096]{1,0:T(8,128)(2,1)} %w2_ref.1, bf16[224,4096]{1,0:T(8,128)(2,1)} %w3_ref.1), custom_call_target="tpu_custom_call" | custom-call | tf_op jit(solution)/shard_map/pallas_call | solution.py:417
  105.6 1.4 %copy.12 = f32[2,4096]{1,0:T(2,128)} copy(f32[2,4096]{1,0:T(2,128)} %get-tuple-element.12) | data formatting | bytes 65536
  107.0 1.2 %copy.13 = f32[2]{0:T(128)} copy(f32[2]{0:T(128)} %get-tuple-element.13) | data formatting | bytes 16
